TPU v7x, 256 devices: a whole 4x4x8 slice. The times are simulated.
256 devices in a mesh: grp: 4 (over z_lo), au: 4 (over z_hi, core), vert: 16 (over y, x).
Axes of the slice: x: 4, y: 4, z: 8 (z_hi: 2, z_lo: 4; z = z_hi * 4 + z_lo), core: 2. Of those that a mesh axis runs over, the one named last changes fastest.
Arguments:
- visibility: float32 [65536, 2], P(('grp', 'au', 'vert')), may hold values from -6 to 6
- destination: int32 [65536, 1], P(('grp', 'au', 'vert')), may hold values from 0 to 63; in each aligned block of 256 rows (0 to 255, 256 to 511, ...) at most 16 rows name the same one
- tile_slot: int32 [65536], P(('grp', 'au', 'vert')), may hold values from 0 to 63
- offsets: int32 [65536, 2], P(('grp', 'au', 'vert')), may hold values from 0 to 120
- taper: float32 [8], replicated, may hold values from 0.2 to 1
Outputs:
- dirty_facet: float32 [512, 512], P(('grp', 'au', 'vert'))
Inputs may be any that keep to these rules, and one draw needn't show every extreme that they name: `destination`: among the rows of one device (aligned blocks of 256 rows) no grid block is named more than 16 times, and in some blocks one is named exactly 16 times. `tile_slot`: A tile number within the owning grid block. `offsets`: the kernel's 8 taps stay inside the tile.
All inputs are finite; a program needn't handle non-finite values.
Results may differ from a plain program's by a relative error of at most 0.0003.
Values sent between devices are 32-bit elements.
A program may use at most 64 MiB of HBM per device.

v0:
```python
import math

import jax
import jax.numpy as jnp
from jax import lax
from jax.sharding import PartitionSpec as P

TILE = 128
SUP = 8
ROWS_DEV = 2048
COLS_DEV = 512
IMG = 512


def matmul(factor_a, factor_b):
    return jnp.dot(
        factor_a, factor_b, precision=lax.Precision.HIGHEST, preferred_element_type=jnp.float32
    )


def phases(pixels, grid_cells, modulus):
    turn_count = pixels[:, None] * (grid_cells[None, :] - modulus // 2) % modulus
    angles = turn_count.astype(jnp.float32) * (2.0 * math.pi / modulus)
    return (jnp.cos(angles), jnp.sin(angles))


def spread(anchor, extent, taper):
    offset = jnp.arange(extent, dtype=jnp.int32)[None, :] - anchor[:, None]
    kernel = jnp.zeros(offset.shape, jnp.float32)
    for tap_index in range(taper.shape[0]):
        kernel = kernel + jnp.where(offset == tap_index, taper[tap_index], 0.0)
    return kernel


def body(visibility, destination, tile_slot, offsets, taper):
    n_rows = lax.axis_size("au")
    n_cols = lax.axis_size("vert")
    owners = n_rows * n_cols
    vis_count = visibility.shape[0]
    capacity = 4 * vis_count // owners
    target = destination[:, 0]
    onehot = (target[:, None] == jnp.arange(owners, dtype=jnp.int32)[None, :]).astype(jnp.int32)
    before = jnp.cumsum(onehot, axis=0) - onehot
    rank_in = jnp.sum(before * onehot, axis=1)
    position = target * capacity + rank_in
    packed = (tile_slot * TILE + offsets[:, 0]) * TILE + offsets[:, 1]
    payload = jnp.concatenate([visibility, packed[:, None].astype(jnp.float32)], axis=1)
    outgoing = jnp.zeros((owners * capacity, 3), jnp.float32).at[position].set(payload)
    incoming = lax.all_to_all(outgoing, ("au", "vert"), split_axis=0, concat_axis=0, tiled=True)
    slot_code = incoming[:, 2].astype(jnp.int32)
    tiles_across = COLS_DEV // TILE
    tile_index = slot_code // (TILE * TILE)
    row_anchor = tile_index // tiles_across * TILE + slot_code // TILE % TILE
    col_anchor = tile_index % tiles_across * TILE + slot_code % TILE
    row_kernel = spread(row_anchor, ROWS_DEV, taper)
    col_kernel = spread(col_anchor, COLS_DEV, taper)
    weighted = jnp.concatenate(
        [incoming[:, 0:1] * col_kernel, incoming[:, 1:2] * col_kernel], axis=1
    )
    gridded = lax.dot_general(
        row_kernel,
        weighted,
        (((0,), (0,)), ((), ())),
        precision=lax.Precision.HIGHEST,
        preferred_element_type=jnp.float32,
    )
    grid_re = gridded[:, :COLS_DEV]
    grid_im = gridded[:, COLS_DEV:]
    total_rows = ROWS_DEV * n_rows
    total_cols = COLS_DEV * n_cols
    row_share = ROWS_DEV
    first_row = lax.axis_index("au") * ROWS_DEV
    pixel_cols = jnp.arange(IMG, dtype=jnp.int32) - IMG // 2
    col_cells = lax.axis_index("vert") * COLS_DEV + jnp.arange(COLS_DEV, dtype=jnp.int32)
    cos_v, sin_v = phases(pixel_cols, col_cells, total_cols)
    part_re = matmul(grid_re, cos_v.T) - matmul(grid_im, sin_v.T)
    part_im = matmul(grid_re, sin_v.T) + matmul(grid_im, cos_v.T)
    row_cells = first_row + jnp.arange(row_share, dtype=jnp.int32)
    normalise = 1.0 / (SUP * math.sqrt(vis_count * lax.axis_size(("grp", "au", "vert"))))

    def facet_rows():
        pixel_rows = (
            jnp.arange(
                IMG // lax.axis_size(("grp", "au", "vert")) * lax.axis_size(("grp", "au", "vert")),
                dtype=jnp.int32,
            )
            - IMG // 2
        )
        cos_u, sin_u = phases(pixel_rows, row_cells, total_rows)
        return (matmul(cos_u, part_re) - matmul(sin_u, part_im)) * normalise

    return lax.psum_scatter(facet_rows(), ("grp", "au", "vert"), scatter_dimension=0, tiled=True)


def solution(mesh):
    return jax.shard_map(
        body,
        mesh=mesh,
        in_specs=(
            P(("grp", "au", "vert"), None),
            P(("grp", "au", "vert"), None),
            P(("grp", "au", "vert")),
            P(("grp", "au", "vert"), None),
            P(),
        ),
        out_specs=P(("grp", "au", "vert"), None),
        check_vma=False,
    )
```

profile of v0, /device:TPU:1, one launch (start us, length us, event | category | flops | bytes accessed | tf_op | source)
XLA Modules:
  0.0 452.5 jit_solution(8823826479852465700)
XLA Ops:
  6.5 0.7 fusion.105
  7.2 0.6 reduce-window.6
  7.8 0.2 slice_reduce_fusion
  8.1 0.8 fusion.104
  8.8 0.7 compare_select_fusion.5
  9.5 0.8 fusion.145
  10.3 0.7 add_convert_fusion
  11.0 0.7 pad_maximum_fusion
  11.7 0.1 copy.13
  11.8 1.3 scatter_custom_fusion
  13.1 1.1 copy.14
  14.2 15.6 %all-to-all-start = ((f32[64,16,3]{1,2,0:T(4,128)}), f32[64,16,3]{1,2,0:T(4,128)S(1)}, u32[]{:S(2)}, u32[]{:S(2)}) async-start(f32[64,16,3]{1,2,0:T(4,128)} %copy.14), calls=%async_computation | async-start | bytes 262144 | tf_op jit(solution)/shard_map/all_to_all | solution.py:49
  29.9 1.6 fusion.146
  31.5 11.5 %all-to-all-done = f32[64,16,3]{1,2,0:T(4,128)S(1)} async-done(((f32[64,16,3]{1,2,0:T(4,128)}), f32[64,16,3]{1,2,0:T(4,128)S(1)}, u32[]{:S(2)}, u32[]{:S(2)}) %all-to-all-start) | async-done | bytes 12320 | tf_op jit(solution)/shard_map/all_to_all | solution.py:49
  43.2 6.8 %fusion.93 = (f32[1024,512]{1,0:T(8,128)S(1)}, f32[1024,512]{1,0:T(8,128)S(1)}) fusion(f32[]{:T(128)} %bitcast.17, f32[]{:T(128)} %bitcast.16, f32[]{:T(128)} %bitcast.15, f32[]{:T(128)} %bitcast.14, f32[]{:T(128)} %bitcast.13, f32[]{:T(128)} %bitcast.12, f32[]{:T(128)} %bitcast.11, f32[]{:T(128)} %bitcast.10, s32[1024]{0:T(1024)S(1)} %bitcast.42, ...), kind=kLoop, calls=%fused_computation.90 | loop fusion | flops 13631488 | bytes 4206624 | tf_op jit(solution)/shard_map/mul | solution.py:58
  50.1 46.0 %fusion = f32[2048,1024]{1,0:T(8,128)S(1)} fusion(f32[1024,512]{1,0:T(8,128)S(1)} %get-tuple-element.10, f32[1024,512]{1,0:T(8,128)S(1)} %get-tuple-element.9, f32[]{:T(128)} %bitcast.17, f32[]{:T(128)} %bitcast.16, f32[]{:T(128)} %bitcast.15, f32[]{:T(128)} %bitcast.14, f32[]{:T(128)} %bitcast.13, f32[]{:T(128)} %bitcast.12, f32[]{:T(128)} %bitcast.11, ...), kind=kOutput, calls=%fused_computation.1 | convolution fusion | flops 25821184000 | bytes 12587040 | tf_op jit(solution)/shard_map/dot_general | solution.py:60
  96.0 10.7 %fusion.62 = f32[2048,512]{1,0:T(8,128)S(1)} fusion(f32[2048,1024]{1,0:T(8,128)S(1)} %fusion, s32[512]{0:T(512)S(1)} %get-tuple-element.21, s32[512]{0:T(512)S(1)} %get-tuple-element.22), kind=kOutput, calls=%fused_computation.61 | convolution fusion | flops 6446120960 | bytes 8392704 | tf_op jit(solution)/shard_map/dot_general | solution.py:16
  106.7 11.3 %fusion.66 = f32[2048,512]{1,0:T(8,128)S(1)} fusion(f32[2048,1024]{1,0:T(8,128)S(1)} %fusion, s32[512]{0:T(512)S(1)} %get-tuple-element.21, s32[512]{0:T(512)S(1)} %get-tuple-element.22), kind=kOutput, calls=%fused_computation.65 | convolution fusion | flops 6446120960 | bytes 8392704 | tf_op jit(solution)/shard_map/dot_general | solution.py:16
  118.1 11.1 %fusion.64 = f32[2048,512]{1,0:T(8,128)S(1)} fusion(f32[2048,1024]{1,0:T(8,128)S(1)} %fusion, s32[512]{0:T(512)S(1)} %get-tuple-element.21, s32[512]{0:T(512)S(1)} %get-tuple-element.22), kind=kOutput, calls=%fused_computation.63 | convolution fusion | flops 6446120960 | bytes 8392704 | tf_op jit(solution)/shard_map/dot_general | solution.py:16
  129.2 11.3 %fusion.68 = f32[2048,512]{1,0:T(8,128)S(1)} fusion(f32[2048,1024]{1,0:T(8,128)S(1)} %fusion, s32[512]{0:T(512)S(1)} %get-tuple-element.21, s32[512]{0:T(512)S(1)} %get-tuple-element.22), kind=kOutput, calls=%fused_computation.67 | convolution fusion | flops 6446120960 | bytes 8392704 | tf_op jit(solution)/shard_map/dot_general | solution.py:16
  140.5 22.9 %fusion.38 = f32[512,512]{1,0:T(8,128)S(1)} fusion(f32[2048,512]{1,0:T(8,128)S(1)} %fusion.66, f32[2048,512]{1,0:T(8,128)S(1)} %fusion.62, s32[2048]{0:T(1024)S(1)} %add_add_fusion, s32[512]{0:T(512)S(1)} %get-tuple-element.22), kind=kOutput, calls=%fused_computation.37 | convolution fusion | flops 6458179584 | bytes 9447424 | tf_op jit(solution)/shard_map/dot_general | solution.py:16
  163.4 23.4 %fusion.85 = f32[512,512]{1,0:T(8,128)} fusion(f32[512,512]{1,0:T(8,128)S(1)} %fusion.38, f32[2048,512]{1,0:T(8,128)S(1)} %fusion.68, f32[2048,512]{1,0:T(8,128)S(1)} %fusion.64, s32[2048]{0:T(1024)S(1)} %add_add_fusion, s32[512]{0:T(512)S(1)} %get-tuple-element.22), kind=kOutput, calls=%fused_computation.85 | convolution fusion | flops 6458703872 | bytes 10496000 | tf_op jit(solution)/shard_map/dot_general | solution.py:16
  186.8 257.3 %all-reduce.3.cloned.1.call-done = f32[512,512]{1,0:T(8,128)} async-done(((f32[512,512]{1,0:T(8,128)}), f32[512,512]{1,0:T(8,128)}) %all-reduce.3.cloned.1.call-update) | async-done | bytes 1048592
  444.1 1.3 constant_dynamic-slice_fusion
  (11 shorter events, 0.3 us)
Async XLA Ops:
  14.2 28.8 %all-to-all-start = ((f32[64,16,3]{1,2,0:T(4,128)}), f32[64,16,3]{1,2,0:T(4,128)S(1)}, u32[]{:S(2)}, u32[]{:S(2)}) async-start(f32[64,16,3]{1,2,0:T(4,128)} %copy.14), calls=%async_computation | async-start | bytes 262144 | tf_op jit(solution)/shard_map/all_to_all | solution.py:49
  29.8 414.3 %all-reduce.3.cloned.1.call-start = ((), (), s32[]{:S(2)}) async-start(), calls=%async_computation.1 | async-start | bytes 2097152
Sparse Core Ops, SparseCore 0:
  186.9 257.1 all-reduce.2
where the time goes:
time: 457 us; the launch traced here: 452 us
  waiting for transfers between devices  269 us (59%)
  matrix products  137 us (30%)
  starting transfers between devices  15.7 us (3%)
  between operations  13.7 us (3%)
  other arithmetic  11.1 us (2%)
  local copies, waits for them, and re-layouts  6.5 us (1%)
    unnamed x2, waiting for transfers between devices  257 us
    dot_general x6, matrix products, matmul(): jnp.dot(factor_a, factor_b, precision=lax.Precision.HIGHEST, preferred_el...  90.7 us
    dot_general x1, matrix products, body(): lax.dot_general(row_kernel, weighted, (((0,), (0,)), ((), ())), precision...  46 us
    all_to_all x1, starting transfers between devices, body(): lax.all_to_all(outgoing, ('au', 'vert'), split_axis=0, concat_axis=0, til...  15.6 us
    all_to_all x1, waiting for transfers between devices, body(): lax.all_to_all(outgoing, ('au', 'vert'), split_axis=0, concat_axis=0, til...  11.5 us
  transfers between devices with their start and end apart: 2, of which 2 were waited for; matrix products, arithmetic and copies ran while one was open for 0% of the time, Pallas kernels for 0%

commit v1 on v0

v1 whole, which is shorter than its diff:
```python
import math

import jax
import jax.numpy as jnp
from jax import lax
from jax.experimental import pallas as pl
from jax.experimental.pallas import tpu as pltpu
from jax.sharding import PartitionSpec as P

TILE = 128
SUP = 8
ROWS_DEV = 2048
COLS_DEV = 512
IMG = 512
CELLS = 8192
MESH = pl.DeviceIdType.MESH

RING = 8
OWN = 32
ROWS = 64
HALF = IMG // 2
VIS = 256


def sincos(turns):
    turns = turns - jnp.floor(turns + 0.5)
    square = turns * turns
    sine = jnp.full_like(turns, -(math.pi**11) / math.factorial(11))
    for order in (9, 7, 5, 3, 1):
        sign = 1.0 if order % 4 == 1 else -1.0
        sine = sine * square + sign * math.pi**order / math.factorial(order)
    sine = sine * turns
    cosine = jnp.full_like(turns, math.pi**12 / math.factorial(12))
    for order in (10, 8, 6, 4, 2, 0):
        sign = 1.0 if order % 4 == 0 else -1.0
        cosine = cosine * square + sign * math.pi**order / math.factorial(order)
    return 1.0 - 2.0 * sine * sine, 2.0 * sine * cosine


def times(a, b):
    return a[0] * b[0] - a[1] * b[1], a[0] * b[1] + a[1] * b[0]


def stack(a, b):
    return jnp.concatenate([a[0], b[0]], axis=0), jnp.concatenate([a[1], b[1]], axis=0)


def split(value):
    high = value.astype(jnp.bfloat16)
    return high, (value - high.astype(jnp.float32)).astype(jnp.bfloat16)


def taper_sum(taper, pixel):
    step = sincos(pixel * (1.0 / CELLS))
    total = (jnp.full_like(pixel, taper[SUP - 1]), jnp.zeros_like(pixel))
    for tap in range(SUP - 2, -1, -1):
        re, im = times(total, step)
        total = (re + taper[tap], im)
    return total


def rows_of(shape):
    return lax.broadcasted_iota(jnp.int32, shape, 0)


def lanes_of(shape):
    return lax.broadcasted_iota(jnp.int32, shape, 1)


def phases(fields, first_pixel, v_ref, w_ref):
    re, im, x, y = (fields[i : i + 1, :] for i in range(4))
    row = rows_of((8, VIS))
    rowf = row.astype(jnp.float32)
    unit = 1.0 / CELLS
    col = sincos((rowf + 0.5) * y * unit)
    line = sincos(((first_pixel + 2.0 * rowf) * x - 0.5 * y) * unit)
    power = jnp.where(row < 5, 8 << jnp.minimum(row, 4), jnp.where(row == 7, 1, 16 << jnp.maximum(row - 5, 0)))
    turn = sincos(power.astype(jnp.float32) * jnp.where(row < 5, y, x) * unit)

    def step(i):
        return turn[0][i : i + 1, :], turn[1][i : i + 1, :]

    line = times((re, im), line)
    tiles = [stack(line, times(line, step(5)))]
    tiles.append(times(tiles[0], step(6)))
    tiles += [times(tile, step(7)) for tile in tiles]
    for i, tile in enumerate(tiles):
        for part in range(2):
            high, low = split(tile[part])
            w_ref[64 * part + 16 * i : 64 * part + 16 * i + 16, :] = high
            w_ref[128 + 64 * part + 16 * i : 128 + 64 * part + 16 * i + 16, :] = low
    tiles = [stack(col, times(col, step(0)))]
    for level in range(1, 5):
        tiles += [times(tile, step(level)) for tile in tiles]
    for i, tile in enumerate(tiles):
        for part in range(2):
            high, low = split(tile[part])
            v_ref[256 * part + 16 * i : 256 * part + 16 * i + 16, 0:VIS] = high
            v_ref[256 * part + 16 * i : 256 * part + 16 * i + 16, VIS : 2 * VIS] = low


def kernel(
    vis_hbm, dest_hbm, slot_hbm, off_hbm, taper_hbm, out_ref,
    vis, dest, slot, off, taper, fields, v_ref, w_ref, acc, tt, sends, recvs,
    load_sem, a_send, a_recv, b_send, b_recv,
):
    grp, au, vert = lax.axis_index("grp"), lax.axis_index("au"), lax.axis_index("vert")
    core = au % 2
    z = (au // 2) * 4 + grp
    y, x = vert // 4, vert % 4

    def ring_peer(offset):
        there = (z + offset) % RING
        return there % 4, (there // 4) * 2 + core, vert

    shifts = [(c, b, a) for c in range(2) for b in range(4) for a in range(4)]
    shifts.sort(key=lambda s: -(min(s[1], 4 - s[1]) + min(s[2], 4 - s[2]) + 0.5 * s[0]))
    shifts = shifts[:-1]

    def own_index(shift):
        return ((core + shift[0]) % 2) * 16 + ((y + shift[1]) % 4) * 4 + (x + shift[2]) % 4

    def own_peer(shift):
        return grp, (au // 2) * 2 + (core + shift[0]) % 2, ((y + shift[1]) % 4) * 4 + (x + shift[2]) % 4

    barrier = pltpu.get_barrier_semaphore()
    for offset in range(1, RING):
        pl.semaphore_signal(barrier, inc=1, device_id=ring_peer(offset), device_id_type=MESH)
    for shift in shifts:
        pl.semaphore_signal(barrier, inc=1, device_id=own_peer(shift), device_id_type=MESH)

    loads = [
        pltpu.make_async_copy(src, dst, load_sem.at[i])
        for i, (src, dst) in enumerate(
            ((vis_hbm, vis), (dest_hbm, dest), (slot_hbm, slot), (off_hbm, off), (taper_hbm, taper))
        )
    ]
    for load in loads:
        load.start()
    for load in loads[:4]:
        load.wait()
    target, tile = dest[...], slot[...]
    row0 = target // 16 * ROWS_DEV + tile // 4 * TILE + off[0:1, :]
    col0 = target % 16 * COLS_DEV + tile % 4 * TILE + off[1:2, :]
    fields[0, 0:2, :] = vis[...]
    fields[0, 2:3, :] = (row0 - CELLS // 2).astype(jnp.float32)
    fields[0, 3:4, :] = (col0 - CELLS // 2).astype(jnp.float32)

    pl.semaphore_wait(barrier, RING - 1 + len(shifts))
    order = [1, 7, 2, 6, 3, 5, 4]
    gathers = {}
    for offset in order[::-1]:
        gathers[offset] = pltpu.make_async_remote_copy(
            src_ref=fields.at[0],
            dst_ref=fields.at[offset],
            send_sem=a_send.at[offset],
            recv_sem=a_recv.at[offset],
            device_id=ring_peer(offset),
            device_id_type=MESH,
        )
        gathers[offset].start()

    position = grp * 2 + au // 2
    first_pixel = (position * ROWS - HALF).astype(jnp.float32)
    loads[4].wait()
    taps = [taper[i] for i in range(SUP)]
    lane = lanes_of((8, 128))
    left = lane < 64
    within = lane % 64
    pixel = first_pixel + (2 * (within % 32) + within // 32).astype(jnp.float32)
    norm = 1.0 / (SUP * math.sqrt(65536))
    line_re, line_im = taper_sum(taps, pixel)
    line_taper = (line_re * norm, line_im * norm)

    def table(i, carry):
        k = (rows_of((8, 128)) + 8 * i).astype(jnp.float32)
        pair = times(taper_sum(taps, jnp.where(left, k, -1.0 - k)), line_taper)
        rows = pl.ds(pl.multiple_of(8 * i, 8), 8)
        tt[0, rows, :] = pair[0]
        tt[1, rows, :] = pair[1]
        return carry

    lax.fori_loop(0, HALF // 8, table, 0)

    for index, offset in enumerate([0] + order):
        if offset:
            gathers[offset].wait_recv()
        phases(fields[offset], first_pixel, v_ref.at[index % 2], w_ref.at[index % 2])
        weights = w_ref[index % 2]
        part = None
        for half in range(2):
            product = lax.dot_general(
                v_ref[index % 2, :, half * VIS : (half + 1) * VIS],
                weights,
                (((1,), (1,)), ((), ())),
                preferred_element_type=jnp.float32,
            )
            part = product if part is None else part + product
        if index == 0:
            acc[...] = part
        else:
            acc[...] += part

    for i in range(2):
        rows = slice(128 * i, 128 * i + 128)
        cos_sum = acc[rows, 0:128] + acc[rows, 128:256]
        rows2 = slice(256 + 128 * i, 256 + 128 * i + 128)
        sin_sum = acc[rows2, 0:128] + acc[rows2, 128:256]
        minus = cos_sum - pltpu.roll(sin_sum, 64, 1)
        plus = pltpu.roll(cos_sum, 64, 1) + sin_sum
        mask = lanes_of((128, 128)) < 64
        facet = tt[0, rows, :] * jnp.where(mask, minus, plus) - tt[1, rows, :] * jnp.where(mask, plus, minus)
        facet = facet.T
        for group in range(4):
            for t in range(4):
                sends[pl.ds(64 * t + 2 * group + i, 8, stride=8), :] = facet[
                    32 * group + 8 * t : 32 * group + 8 * t + 8, :
                ]

    exchanges = []
    for i, shift in enumerate(shifts):
        start = pl.multiple_of(8 * own_index(shift), 8)
        exchanges.append(
            pltpu.make_async_remote_copy(
                src_ref=sends.at[pl.ds(start, 8), :],
                dst_ref=recvs.at[i],
                send_sem=b_send.at[i],
                recv_sem=b_recv.at[i],
                device_id=own_peer(shift),
                device_id_type=MESH,
            )
        )
        exchanges[-1].start()
    mine = pl.multiple_of(8 * (core * 16 + vert), 8)
    total = sends[pl.ds(mine, 8), :]
    for i in range(len(shifts) - 1, -1, -1):
        exchanges[i].wait_recv()
        total = total + recvs[i]
    mirrored = jnp.take_along_axis(total, 127 - lane, axis=1)
    for e in range(2):
        for h in range(2):
            out_ref[e : e + 1, 256 + 128 * h : 384 + 128 * h] = total[2 * e + h : 2 * e + h + 1, :]
            out_ref[e : e + 1, 128 * (1 - h) : 128 * (2 - h)] = mirrored[4 + 2 * e + h : 5 + 2 * e + h, :]
    for offset in order:
        gathers[offset].wait_send()
    for exchange in exchanges:
        exchange.wait_send()


def body(visibility, destination, tile_slot, offsets, taper):
    any_space = pl.BlockSpec(memory_space=pl.ANY)
    return pl.pallas_call(
        kernel,
        out_shape=jax.ShapeDtypeStruct((2, IMG), jnp.float32),
        in_specs=[any_space] * 5,
        out_specs=pl.BlockSpec(memory_space=pltpu.VMEM),
        scratch_shapes=[
            pltpu.VMEM((2, VIS), jnp.float32),
            pltpu.VMEM((1, VIS), jnp.int32),
            pltpu.VMEM((1, VIS), jnp.int32),
            pltpu.VMEM((2, VIS), jnp.int32),
            pltpu.SMEM((SUP,), jnp.float32),
            pltpu.VMEM((RING, 4, VIS), jnp.float32),
            pltpu.VMEM((2, IMG, 2 * VIS), jnp.bfloat16),
            pltpu.VMEM((2, 4 * ROWS, VIS), jnp.bfloat16),
            pltpu.VMEM((IMG, 4 * ROWS), jnp.float32),
            pltpu.VMEM((2, HALF, 128), jnp.float32),
            pltpu.VMEM((OWN * 8, 128), jnp.float32),
            pltpu.VMEM((OWN - 1, 8, 128), jnp.float32),
            pltpu.SemaphoreType.DMA((5,)),
            pltpu.SemaphoreType.DMA((RING,)),
            pltpu.SemaphoreType.DMA((RING,)),
            pltpu.SemaphoreType.DMA((OWN - 1,)),
            pltpu.SemaphoreType.DMA((OWN - 1,)),
        ],
        compiler_params=pltpu.CompilerParams(collective_id=0, has_side_effects=True),
    )(visibility.T, destination.T, tile_slot.reshape(1, -1), offsets.T, taper)


def solution(mesh):
    return jax.shard_map(
        body,
        mesh=mesh,
        in_specs=(
            P(("grp", "au", "vert"), None),
            P(("grp", "au", "vert"), None),
            P(("grp", "au", "vert")),
            P(("grp", "au", "vert"), None),
            P(),
        ),
        out_specs=P(("grp", "au", "vert"), None),
        check_vma=False,
    )
```

time: 457 us -> 23.7 us (0.05)
  waiting for transfers between devices: 269 us -> 0 us
  matrix products: 137 us -> 0 us
  Pallas kernels: 0 us -> 22.3 us
  starting transfers between devices: 15.7 us -> 0 us
  between operations: 13.7 us -> 0.01 us
  other arithmetic: 11.1 us -> 0 us
  local copies, waits for them, and re-layouts: 6.5 us -> 1.28 us
    unnamed x2 -> x0, waiting for transfers between devices: 257 us -> none
    dot_general x7 -> x0, matrix products: 137 us -> none  [the longest x6 90.7 us: matmul(): jnp.dot(factor_a, factor_b, precision=lax.Precision.HIGHEST, preferred_el...]
    pallas_call x0 -> x1, Pallas kernels: none -> 22.3 us  [body(): pl.pallas_call(kernel, out_shape=jax.ShapeDtypeStruct((2, IMG), jnp.float...]
    all_to_all x1 -> x0, starting transfers between devices: 15.6 us -> none  [body(): lax.all_to_all(outgoing, ('au', 'vert'), split_axis=0, concat_axis=0, til...]
    all_to_all x1 -> x0, waiting for transfers between devices: 11.5 us -> none  [body(): lax.all_to_all(outgoing, ('au', 'vert'), split_axis=0, concat_axis=0, til...]
    mul x1 -> x0, other arithmetic: 6.83 us -> none  [body(): incoming[:, 0:1] * col_kernel]
  transfers between devices with their start and end apart: 2 -> 0, of which waited for: 2 -> 0; matrix products, arithmetic and copies ran while one was open for 0% -> 0% of each run, Pallas kernels for 0% -> 0%
where the time goes in v1:
time: 23.7 us; the launch traced here: 23.6 us
  Pallas kernels  22.3 us (94%)
  local copies, waits for them, and re-layouts  1.28 us (5%)
    pallas_call x1, Pallas kernels, body(): pl.pallas_call(kernel, out_shape=jax.ShapeDtypeStruct((2, IMG), jnp.float...  22.3 us
    unnamed x1, local copies, waits for them, and re-layouts  1.28 us

profile of v1, /device:TPU:1, one launch (start us, length us, event | category | flops | bytes accessed | tf_op | source)
XLA Modules:
  0.0 23.6 jit_solution(7652402827906711634)
XLA Ops:
  0.0 22.3 %shard_map.55 = f32[2,512]{1,0:T(2,128)} custom-call(f32[2,256]{1,0:T(2,128)} %bitcast.4, s32[1,256]{1,0:T(1,128)} %bitcast.6, s32[1,256]{1,0:T(1,128)} %bitcast.7, s32[2,256]{1,0:T(2,128)} %bitcast.5, f32[8]{0:T(128)} %taper_hbm.1), custom_call_target="tpu_custom_call" | custom-call | tf_op jit(solution)/shard_map/pallas_call | solution.py:252
  22.3 1.3 %copy.7 = f32[2,512]{1,0:T(2,128)} copy(f32[2,512]{1,0:T(2,128)} %shard_map.55) | data formatting | bytes 8192

commit v2 on v1

--- a/solution.py
+++ b/solution.py
@@ -101,8 +101,8 @@
 
 def kernel(
     vis_hbm, dest_hbm, slot_hbm, off_hbm, taper_hbm, out_ref,
-    vis, dest, slot, off, taper, fields, v_ref, w_ref, acc, tt, sends, recvs,
-    load_sem, a_send, a_recv, b_send, b_recv,
+    vis, dest, slot, off, taper, fields, v_ref, w_ref, acc, sends, recvs,
+    load_sem, a_send, a_recv, b_send, b_recv, plane_sem, pair_sem,
 ):
     grp, au, vert = lax.axis_index("grp"), lax.axis_index("au"), lax.axis_index("vert")
     core = au % 2
@@ -117,17 +117,22 @@
     shifts.sort(key=lambda s: -(min(s[1], 4 - s[1]) + min(s[2], 4 - s[2]) + 0.5 * s[0]))
     shifts = shifts[:-1]
 
-    def own_index(shift):
-        return ((core + shift[0]) % 2) * 16 + ((y + shift[1]) % 4) * 4 + (x + shift[2]) % 4
+    def own_vert(shift):
+        return ((y + shift[1]) % 4) * 4 + (x + shift[2]) % 4
 
     def own_peer(shift):
-        return grp, (au // 2) * 2 + (core + shift[0]) % 2, ((y + shift[1]) % 4) * 4 + (x + shift[2]) % 4
-
+        return grp, (au // 2) * 2 + (core + shift[0]) % 2, own_vert(shift)
+
+    def signal(sem, peers):
+        for peer in peers:
+            pl.semaphore_signal(sem, inc=1, device_id=peer, device_id_type=MESH)
+
+    row = [own_peer((0, 0, a)) for a in range(1, 4)]
+    column = [own_peer((0, b, 0)) for b in range(1, 4)]
+    pair = own_peer((1, 0, 0))
+    ring = [ring_peer(offset) for offset in range(1, RING)]
     barrier = pltpu.get_barrier_semaphore()
-    for offset in range(1, RING):
-        pl.semaphore_signal(barrier, inc=1, device_id=ring_peer(offset), device_id_type=MESH)
-    for shift in shifts:
-        pl.semaphore_signal(barrier, inc=1, device_id=own_peer(shift), device_id_type=MESH)
+    signal(barrier, ring + row + column + [pair])
 
     loads = [
         pltpu.make_async_copy(src, dst, load_sem.at[i])
@@ -146,7 +151,7 @@
     fields[0, 2:3, :] = (row0 - CELLS // 2).astype(jnp.float32)
     fields[0, 3:4, :] = (col0 - CELLS // 2).astype(jnp.float32)
 
-    pl.semaphore_wait(barrier, RING - 1 + len(shifts))
+    pl.semaphore_wait(barrier, len(ring + row + column) + 1)
     order = [1, 7, 2, 6, 3, 5, 4]
     gathers = {}
     for offset in order[::-1]:
@@ -159,33 +164,12 @@
             device_id_type=MESH,
         )
         gathers[offset].start()
+    signal(plane_sem, row + [pair])
 
     position = grp * 2 + au // 2
     first_pixel = (position * ROWS - HALF).astype(jnp.float32)
-    loads[4].wait()
-    taps = [taper[i] for i in range(SUP)]
-    lane = lanes_of((8, 128))
-    left = lane < 64
-    within = lane % 64
-    pixel = first_pixel + (2 * (within % 32) + within // 32).astype(jnp.float32)
-    norm = 1.0 / (SUP * math.sqrt(65536))
-    line_re, line_im = taper_sum(taps, pixel)
-    line_taper = (line_re * norm, line_im * norm)
-
-    def table(i, carry):
-        k = (rows_of((8, 128)) + 8 * i).astype(jnp.float32)
-        pair = times(taper_sum(taps, jnp.where(left, k, -1.0 - k)), line_taper)
-        rows = pl.ds(pl.multiple_of(8 * i, 8), 8)
-        tt[0, rows, :] = pair[0]
-        tt[1, rows, :] = pair[1]
-        return carry
-
-    lax.fori_loop(0, HALF // 8, table, 0)
-
-    for index, offset in enumerate([0] + order):
-        if offset:
-            gathers[offset].wait_recv()
-        phases(fields[offset], first_pixel, v_ref.at[index % 2], w_ref.at[index % 2])
+
+    def project(index):
         weights = w_ref[index % 2]
         part = None
         for half in range(2):
@@ -201,25 +185,46 @@
         else:
             acc[...] += part
 
+    phases(fields[0], first_pixel, v_ref.at[0], w_ref.at[0])
+    loads[4].wait()
+    taps = [taper[i] for i in range(SUP)]
+    lane, level = lanes_of((8, 128)), rows_of((8, 128))
+    within = lane % 64
+    line_re, line_im = taper_sum(taps, first_pixel + (2 * (within % 32) + within // 32).astype(jnp.float32))
+    norm = 1.0 / (SUP * math.sqrt(65536))
+    line_re, line_im = line_re[0:1, :] * norm, line_im[0:1, :] * norm
+    column_pixel = lane + 128 * (level % 2)
+    col_re, col_im = taper_sum(taps, jnp.where(level < 2, column_pixel, -1 - column_pixel).astype(jnp.float32))
+    pl.semaphore_wait(plane_sem, len(row) + 1)
+    signal(pair_sem, [pair])
+
+    for index, offset in enumerate(order, 1):
+        gathers[offset].wait_recv()
+        project(index - 1)
+        phases(fields[offset], first_pixel, v_ref.at[index % 2], w_ref.at[index % 2])
+    project(RING - 1)
+
     for i in range(2):
         rows = slice(128 * i, 128 * i + 128)
         cos_sum = acc[rows, 0:128] + acc[rows, 128:256]
-        rows2 = slice(256 + 128 * i, 256 + 128 * i + 128)
-        sin_sum = acc[rows2, 0:128] + acc[rows2, 128:256]
+        rows = slice(256 + 128 * i, 256 + 128 * i + 128)
+        sin_sum = acc[rows, 0:128] + acc[rows, 128:256]
         minus = cos_sum - pltpu.roll(sin_sum, 64, 1)
         plus = pltpu.roll(cos_sum, 64, 1) + sin_sum
         mask = lanes_of((128, 128)) < 64
-        facet = tt[0, rows, :] * jnp.where(mask, minus, plus) - tt[1, rows, :] * jnp.where(mask, plus, minus)
-        facet = facet.T
+        real, imag = jnp.where(mask, minus, plus), jnp.where(mask, plus, minus)
+        real, imag = (line_re * real - line_im * imag).T, (line_re * imag + line_im * real).T
         for group in range(4):
+            part = slice(32 * group, 32 * group + 32)
+            tap = slice(group // 2 * 2 + i, group // 2 * 2 + i + 1)
+            facet = col_re[tap, :] * real[part, :] - col_im[tap, :] * imag[part, :]
             for t in range(4):
-                sends[pl.ds(64 * t + 2 * group + i, 8, stride=8), :] = facet[
-                    32 * group + 8 * t : 32 * group + 8 * t + 8, :
-                ]
-
+                sends[pl.ds(64 * t + 2 * group + i, 8, stride=8), :] = facet[8 * t : 8 * t + 8, :]
+
+    pl.semaphore_wait(pair_sem, 1)
     exchanges = []
     for i, shift in enumerate(shifts):
-        start = pl.multiple_of(8 * own_index(shift), 8)
+        start = pl.multiple_of(8 * ((core + shift[0]) % 2 * 16 + own_vert(shift)), 8)
         exchanges.append(
             pltpu.make_async_remote_copy(
                 src_ref=sends.at[pl.ds(start, 8), :],
@@ -233,6 +238,8 @@
         exchanges[-1].start()
     mine = pl.multiple_of(8 * (core * 16 + vert), 8)
     total = sends[pl.ds(mine, 8), :]
+    for offset in order:
+        gathers[offset].wait_send()
     for i in range(len(shifts) - 1, -1, -1):
         exchanges[i].wait_recv()
         total = total + recvs[i]
@@ -241,8 +248,6 @@
         for h in range(2):
             out_ref[e : e + 1, 256 + 128 * h : 384 + 128 * h] = total[2 * e + h : 2 * e + h + 1, :]
             out_ref[e : e + 1, 128 * (1 - h) : 128 * (2 - h)] = mirrored[4 + 2 * e + h : 5 + 2 * e + h, :]
-    for offset in order:
-        gathers[offset].wait_send()
     for exchange in exchanges:
         exchange.wait_send()
 
@@ -251,7 +256,7 @@
     any_space = pl.BlockSpec(memory_space=pl.ANY)
     return pl.pallas_call(
         kernel,
-        out_shape=jax.ShapeDtypeStruct((2, IMG), jnp.float32),
+        out_shape=pltpu.VMEM((2, IMG), jnp.float32),
         in_specs=[any_space] * 5,
         out_specs=pl.BlockSpec(memory_space=pltpu.VMEM),
         scratch_shapes=[
@@ -264,7 +269,6 @@
             pltpu.VMEM((2, IMG, 2 * VIS), jnp.bfloat16),
             pltpu.VMEM((2, 4 * ROWS, VIS), jnp.bfloat16),
             pltpu.VMEM((IMG, 4 * ROWS), jnp.float32),
-            pltpu.VMEM((2, HALF, 128), jnp.float32),
             pltpu.VMEM((OWN * 8, 128), jnp.float32),
             pltpu.VMEM((OWN - 1, 8, 128), jnp.float32),
             pltpu.SemaphoreType.DMA((5,)),
@@ -272,6 +276,8 @@
             pltpu.SemaphoreType.DMA((RING,)),
             pltpu.SemaphoreType.DMA((OWN - 1,)),
             pltpu.SemaphoreType.DMA((OWN - 1,)),
+            pltpu.SemaphoreType.REGULAR,
+            pltpu.SemaphoreType.REGULAR,
         ],
         compiler_params=pltpu.CompilerParams(collective_id=0, has_side_effects=True),
     )(visibility.T, destination.T, tile_slot.reshape(1, -1), offsets.T, taper)

time: 23.7 us -> 22.7 us (0.958)
  local copies, waits for them, and re-layouts: 1.28 us -> 0.6 us
  Pallas kernels: 22.3 us -> 22 us
    unnamed x1, local copies, waits for them, and re-layouts: 1.28 us -> 0.6 us
where the time goes in v2:
time: 22.7 us
  Pallas kernels  22 us (97%)
  local copies, waits for them, and re-layouts  0.6 us (3%)
    pallas_call x1, Pallas kernels, body(): pl.pallas_call(kernel, out_shape=pltpu.VMEM((2, IMG), jnp.float32), in_sp...  22 us
    unnamed x1, local copies, waits for them, and re-layouts  0.6 us

profile of v2, /device:TPU:1, one launch (start us, length us, event | category | flops | bytes accessed | tf_op | source)
XLA Modules:
  0.0 22.7 jit_solution(17514165255236400714)
XLA Ops:
  0.0 22.0 %shard_map.55 = f32[2,512]{1,0:T(2,128)S(1)} custom-call(f32[2,256]{1,0:T(2,128)} %bitcast.4, s32[1,256]{1,0:T(1,128)} %bitcast.6, s32[1,256]{1,0:T(1,128)} %bitcast.7, s32[2,256]{1,0:T(2,128)} %bitcast.5, f32[8]{0:T(128)} %taper_hbm.1), custom_call_target="tpu_custom_call" | custom-call | tf_op jit(solution)/shard_map/pallas_call | solution.py:257
  22.1 0.6 %copy.7 = f32[2,512]{1,0:T(2,128)} copy(f32[2,512]{1,0:T(2,128)S(1)} %shard_map.55) | data formatting | bytes 8192

commit v3 on v2

--- a/solution.py
+++ b/solution.py
@@ -152,13 +152,13 @@
     fields[0, 3:4, :] = (col0 - CELLS // 2).astype(jnp.float32)
 
     pl.semaphore_wait(barrier, len(ring + row + column) + 1)
-    order = [1, 7, 2, 6, 3, 5, 4]
+    order = [7, 6, 5, 1, 2, 3, 4]
     gathers = {}
     for offset in order[::-1]:
         gathers[offset] = pltpu.make_async_remote_copy(
             src_ref=fields.at[0],
             dst_ref=fields.at[offset],
-            send_sem=a_send.at[offset],
+            send_sem=a_send,
             recv_sem=a_recv.at[offset],
             device_id=ring_peer(offset),
             device_id_type=MESH,
@@ -195,12 +195,13 @@
     line_re, line_im = line_re[0:1, :] * norm, line_im[0:1, :] * norm
     column_pixel = lane + 128 * (level % 2)
     col_re, col_im = taper_sum(taps, jnp.where(level < 2, column_pixel, -1 - column_pixel).astype(jnp.float32))
-    pl.semaphore_wait(plane_sem, len(row) + 1)
-    signal(pair_sem, [pair])
 
     for index, offset in enumerate(order, 1):
         gathers[offset].wait_recv()
         project(index - 1)
+        if index == 4:
+            pl.semaphore_wait(plane_sem, len(row) + 1)
+            signal(pair_sem, [pair])
         phases(fields[offset], first_pixel, v_ref.at[index % 2], w_ref.at[index % 2])
     project(RING - 1)
 
@@ -222,34 +223,34 @@
                 sends[pl.ds(64 * t + 2 * group + i, 8, stride=8), :] = facet[8 * t : 8 * t + 8, :]
 
     pl.semaphore_wait(pair_sem, 1)
-    exchanges = []
     for i, shift in enumerate(shifts):
         start = pl.multiple_of(8 * ((core + shift[0]) % 2 * 16 + own_vert(shift)), 8)
-        exchanges.append(
-            pltpu.make_async_remote_copy(
-                src_ref=sends.at[pl.ds(start, 8), :],
-                dst_ref=recvs.at[i],
-                send_sem=b_send.at[i],
-                recv_sem=b_recv.at[i],
-                device_id=own_peer(shift),
-                device_id_type=MESH,
-            )
-        )
-        exchanges[-1].start()
+        pltpu.make_async_remote_copy(
+            src_ref=sends.at[pl.ds(start, 8), :],
+            dst_ref=recvs.at[i],
+            send_sem=b_send,
+            recv_sem=b_recv,
+            device_id=own_peer(shift),
+            device_id_type=MESH,
+        ).start()
     mine = pl.multiple_of(8 * (core * 16 + vert), 8)
     total = sends[pl.ds(mine, 8), :]
-    for offset in order:
-        gathers[offset].wait_send()
-    for i in range(len(shifts) - 1, -1, -1):
-        exchanges[i].wait_recv()
+    batch = pltpu.make_async_remote_copy(
+        src_ref=recvs, dst_ref=recvs, send_sem=b_send, recv_sem=b_recv, device_id=pair, device_id_type=MESH
+    )
+    batch.wait_recv()
+    for i in range(len(shifts)):
         total = total + recvs[i]
     mirrored = jnp.take_along_axis(total, 127 - lane, axis=1)
     for e in range(2):
         for h in range(2):
             out_ref[e : e + 1, 256 + 128 * h : 384 + 128 * h] = total[2 * e + h : 2 * e + h + 1, :]
             out_ref[e : e + 1, 128 * (1 - h) : 128 * (2 - h)] = mirrored[4 + 2 * e + h : 5 + 2 * e + h, :]
-    for exchange in exchanges:
-        exchange.wait_send()
+    batch.wait_send()
+    rest = fields.at[pl.ds(1, RING - 1)]
+    pltpu.make_async_remote_copy(
+        src_ref=rest, dst_ref=rest, send_sem=a_send, recv_sem=a_recv.at[0], device_id=pair, device_id_type=MESH
+    ).wait_send()
 
 
 def body(visibility, destination, tile_slot, offsets, taper):
@@ -272,10 +273,10 @@
             pltpu.VMEM((OWN * 8, 128), jnp.float32),
             pltpu.VMEM((OWN - 1, 8, 128), jnp.float32),
             pltpu.SemaphoreType.DMA((5,)),
+            pltpu.SemaphoreType.DMA,
             pltpu.SemaphoreType.DMA((RING,)),
-            pltpu.SemaphoreType.DMA((RING,)),
-            pltpu.SemaphoreType.DMA((OWN - 1,)),
-            pltpu.SemaphoreType.DMA((OWN - 1,)),
+            pltpu.SemaphoreType.DMA,
+            pltpu.SemaphoreType.DMA,
             pltpu.SemaphoreType.REGULAR,
             pltpu.SemaphoreType.REGULAR,
         ],

time: 22.7 us -> 22.6 us (level)
  no operation moved by 1% of the time
where the time goes in v3:
time: 22.6 us; the launch traced here: 22.5 us
  Pallas kernels  21.9 us (97%)
  local copies, waits for them, and re-layouts  0.6 us (3%)
    pallas_call x1, Pallas kernels, body(): pl.pallas_call(kernel, out_shape=pltpu.VMEM((2, IMG), jnp.float32), in_sp...  21.9 us
    unnamed x1, local copies, waits for them, and re-layouts  0.6 us

profile of v3, /device:TPU:1, one launch (start us, length us, event | category | flops | bytes accessed | tf_op | source)
XLA Modules:
  0.0 22.5 jit_solution(8795449649332406177)
XLA Ops:
  0.0 21.9 %shard_map.55 = f32[2,512]{1,0:T(2,128)S(1)} custom-call(f32[2,256]{1,0:T(2,128)} %bitcast.4, s32[1,256]{1,0:T(1,128)} %bitcast.6, s32[1,256]{1,0:T(1,128)} %bitcast.7, s32[2,256]{1,0:T(2,128)} %bitcast.5, f32[8]{0:T(128)} %taper_hbm.1), custom_call_target="tpu_custom_call" | custom-call | tf_op jit(solution)/shard_map/pallas_call | solution.py:258
  21.9 0.6 %copy.7 = f32[2,512]{1,0:T(2,128)} copy(f32[2,512]{1,0:T(2,128)S(1)} %shard_map.55) | data formatting | bytes 8192

commit v4 on v3

--- a/solution.py
+++ b/solution.py
@@ -102,16 +102,12 @@
 def kernel(
     vis_hbm, dest_hbm, slot_hbm, off_hbm, taper_hbm, out_ref,
     vis, dest, slot, off, taper, fields, v_ref, w_ref, acc, sends, recvs,
-    load_sem, a_send, a_recv, b_send, b_recv, plane_sem, pair_sem,
+    load_sem, a_send, a_recv, b_send, b_recv, rounds, late_sem,
 ):
     grp, au, vert = lax.axis_index("grp"), lax.axis_index("au"), lax.axis_index("vert")
-    core = au % 2
-    z = (au // 2) * 4 + grp
+    core, half = au % 2, au // 2
+    z = half * 4 + grp
     y, x = vert // 4, vert % 4
-
-    def ring_peer(offset):
-        there = (z + offset) % RING
-        return there % 4, (there // 4) * 2 + core, vert
 
     shifts = [(c, b, a) for c in range(2) for b in range(4) for a in range(4)]
     shifts.sort(key=lambda s: -(min(s[1], 4 - s[1]) + min(s[2], 4 - s[2]) + 0.5 * s[0]))
@@ -121,18 +117,57 @@
         return ((y + shift[1]) % 4) * 4 + (x + shift[2]) % 4
 
     def own_peer(shift):
-        return grp, (au // 2) * 2 + (core + shift[0]) % 2, own_vert(shift)
-
-    def signal(sem, peers):
-        for peer in peers:
-            pl.semaphore_signal(sem, inc=1, device_id=peer, device_id_type=MESH)
-
-    row = [own_peer((0, 0, a)) for a in range(1, 4)]
-    column = [own_peer((0, b, 0)) for b in range(1, 4)]
+        return grp, half * 2 + (core + shift[0]) % 2, own_vert(shift)
+
+    def signal(sem, peer):
+        pl.semaphore_signal(sem, inc=1, device_id=peer, device_id_type=MESH)
+
+    def near(step):
+        return (grp + step) % 4, au, vert
+
+    def across(there):
+        return there, (1 - half) * 2 + core, vert
+
+    def inside(step):
+        return (grp + step >= 0) & (grp + step < 4)
+
     pair = own_peer((1, 0, 0))
-    ring = [ring_peer(offset) for offset in range(1, RING)]
+    plane = [own_peer((0, 0, 1)), own_peer((0, 0, 3)), own_peer((0, 1, 0)), own_peer((0, 3, 0)), pair]
+    neighbours = len(plane) + inside(1).astype(jnp.int32) + inside(-1).astype(jnp.int32)
+
+    def signal_near(sem):
+        for peer in plane:
+            signal(sem, peer)
+        for step in (1, -1):
+
+            @pl.when(inside(step))
+            def _():
+                signal(sem, near(step))
+
+    def gather(peer):
+        pltpu.make_async_remote_copy(
+            src_ref=fields.at[z],
+            dst_ref=fields.at[z],
+            send_sem=a_send,
+            recv_sem=a_recv.at[z],
+            device_id=peer,
+            device_id_type=MESH,
+        ).start()
+
+    def gather_near(distance):
+        for step in (distance, -distance):
+
+            @pl.when(inside(step))
+            def _():
+                gather(near(step))
+
     barrier = pltpu.get_barrier_semaphore()
-    signal(barrier, ring + row + column + [pair])
+    signal_near(barrier)
+
+    @pl.when(half == 0)
+    def _():
+        for there in range(4):
+            signal(barrier, across(there))
 
     loads = [
         pltpu.make_async_copy(src, dst, load_sem.at[i])
@@ -147,34 +182,30 @@
     target, tile = dest[...], slot[...]
     row0 = target // 16 * ROWS_DEV + tile // 4 * TILE + off[0:1, :]
     col0 = target % 16 * COLS_DEV + tile % 4 * TILE + off[1:2, :]
-    fields[0, 0:2, :] = vis[...]
-    fields[0, 2:3, :] = (row0 - CELLS // 2).astype(jnp.float32)
-    fields[0, 3:4, :] = (col0 - CELLS // 2).astype(jnp.float32)
-
-    pl.semaphore_wait(barrier, len(ring + row + column) + 1)
-    order = [7, 6, 5, 1, 2, 3, 4]
-    gathers = {}
-    for offset in order[::-1]:
-        gathers[offset] = pltpu.make_async_remote_copy(
-            src_ref=fields.at[0],
-            dst_ref=fields.at[offset],
-            send_sem=a_send,
-            recv_sem=a_recv.at[offset],
-            device_id=ring_peer(offset),
-            device_id_type=MESH,
-        )
-        gathers[offset].start()
-    signal(plane_sem, row + [pair])
-
-    position = grp * 2 + au // 2
+    fields[z, 0:2, :] = vis[...]
+    fields[z, 2:3, :] = (row0 - CELLS // 2).astype(jnp.float32)
+    fields[z, 3:4, :] = (col0 - CELLS // 2).astype(jnp.float32)
+
+    pl.semaphore_wait(barrier, neighbours + 4 * half)
+
+    @pl.when(half == 1)
+    def _():
+        for there in range(4):
+            gather(across(there))
+        for there in range(4):
+            signal(late_sem, across(there))
+
+    gather_near(1)
+    signal_near(rounds.at[0])
+    position = grp * 2 + half
     first_pixel = (position * ROWS - HALF).astype(jnp.float32)
 
     def project(index):
         weights = w_ref[index % 2]
         part = None
-        for half in range(2):
+        for low in range(2):
             product = lax.dot_general(
-                v_ref[index % 2, :, half * VIS : (half + 1) * VIS],
+                v_ref[index % 2, :, low * VIS : (low + 1) * VIS],
                 weights,
                 (((1,), (1,)), ((), ())),
                 preferred_element_type=jnp.float32,
@@ -185,7 +216,7 @@
         else:
             acc[...] += part
 
-    phases(fields[0], first_pixel, v_ref.at[0], w_ref.at[0])
+    phases(fields[z], first_pixel, v_ref.at[0], w_ref.at[0])
     loads[4].wait()
     taps = [taper[i] for i in range(SUP)]
     lane, level = lanes_of((8, 128)), rows_of((8, 128))
@@ -195,16 +226,36 @@
     line_re, line_im = line_re[0:1, :] * norm, line_im[0:1, :] * norm
     column_pixel = lane + 128 * (level % 2)
     col_re, col_im = taper_sum(taps, jnp.where(level < 2, column_pixel, -1 - column_pixel).astype(jnp.float32))
-
-    for index, offset in enumerate(order, 1):
-        gathers[offset].wait_recv()
+    for distance in (2, 3):
+        pl.semaphore_wait(rounds.at[distance - 2], neighbours)
+        gather_near(distance)
+        signal_near(rounds.at[distance - 1])
+    for index in range(1, RING):
+        if index < 4:
+            source = half * 4 + (grp + index) % 4
+        else:
+            source = (1 - half) * 4 + (grp + 7 - index) % 4
+        pltpu.make_async_remote_copy(
+            src_ref=fields.at[source],
+            dst_ref=fields.at[source],
+            send_sem=a_send,
+            recv_sem=a_recv.at[source],
+            device_id=pair,
+            device_id_type=MESH,
+        ).wait_recv()
         project(index - 1)
-        if index == 4:
-            pl.semaphore_wait(plane_sem, len(row) + 1)
-            signal(pair_sem, [pair])
-        phases(fields[offset], first_pixel, v_ref.at[index % 2], w_ref.at[index % 2])
+        phases(fields[source], first_pixel, v_ref.at[index % 2], w_ref.at[index % 2])
+        if index == 3:
+            pl.semaphore_wait(rounds.at[2], neighbours)
+            signal_near(rounds.at[3])
+
+            @pl.when(half == 0)
+            def _():
+                pl.semaphore_wait(late_sem, 4)
+                for there in range(4):
+                    gather(across(there))
+
     project(RING - 1)
-
     for i in range(2):
         rows = slice(128 * i, 128 * i + 128)
         cos_sum = acc[rows, 0:128] + acc[rows, 128:256]
@@ -222,7 +273,7 @@
             for t in range(4):
                 sends[pl.ds(64 * t + 2 * group + i, 8, stride=8), :] = facet[8 * t : 8 * t + 8, :]
 
-    pl.semaphore_wait(pair_sem, 1)
+    pl.semaphore_wait(rounds.at[3], neighbours)
     for i, shift in enumerate(shifts):
         start = pl.multiple_of(8 * ((core + shift[0]) % 2 * 16 + own_vert(shift)), 8)
         pltpu.make_async_remote_copy(
@@ -277,7 +328,7 @@
             pltpu.SemaphoreType.DMA((RING,)),
             pltpu.SemaphoreType.DMA,
             pltpu.SemaphoreType.DMA,
-            pltpu.SemaphoreType.REGULAR,
+            pltpu.SemaphoreType.REGULAR((4,)),
             pltpu.SemaphoreType.REGULAR,
         ],
         compiler_params=pltpu.CompilerParams(collective_id=0, has_side_effects=True),

time: 22.6 us -> 22.5 us (level)
  no operation moved by 1% of the time
where the time goes in v4:
time: 22.5 us; the launch traced here: 22.4 us
  Pallas kernels  21.8 us (97%)
  local copies, waits for them, and re-layouts  0.6 us (3%)
    pallas_call x1, Pallas kernels, body(): pl.pallas_call(kernel, out_shape=pltpu.VMEM((2, IMG), jnp.float32), in_sp...  21.8 us
    unnamed x1, local copies, waits for them, and re-layouts  0.6 us

profile of v4, /device:TPU:1, one launch (start us, length us, event | category | flops | bytes accessed | tf_op | source)
XLA Modules:
  0.0 22.4 jit_solution(2348477915167928391)
XLA Ops:
  0.0 21.8 %shard_map.55 = f32[2,512]{1,0:T(2,128)S(1)} custom-call(f32[2,256]{1,0:T(2,128)} %bitcast.4, s32[1,256]{1,0:T(1,128)} %bitcast.6, s32[1,256]{1,0:T(1,128)} %bitcast.7, s32[2,256]{1,0:T(2,128)} %bitcast.5, f32[8]{0:T(128)} %taper_hbm.1), custom_call_target="tpu_custom_call" | custom-call | tf_op jit(solution)/shard_map/pallas_call | solution.py:309
  21.8 0.6 %copy.7 = f32[2,512]{1,0:T(2,128)} copy(f32[2,512]{1,0:T(2,128)S(1)} %shard_map.55) | data formatting | bytes 8192

commit v5 on v4

--- a/solution.py
+++ b/solution.py
@@ -20,6 +20,17 @@
 ROWS = 64
 HALF = IMG // 2
 VIS = 256
+
+ORDER = (
+    (1, 2, 3, 7, 6, 5, 4),
+    (2, 3, 0, 7, 4, 6, 5),
+    (3, 1, 0, 4, 5, 7, 6),
+    (4, 5, 6, 7, 2, 1, 0),
+    (5, 6, 7, 3, 2, 1, 0),
+    (6, 7, 4, 3, 2, 1, 0),
+    (7, 5, 4, 3, 0, 2, 1),
+    (6, 5, 4, 0, 3, 1, 2),
+)
 
 
 def sincos(turns):
@@ -102,7 +113,7 @@
 def kernel(
     vis_hbm, dest_hbm, slot_hbm, off_hbm, taper_hbm, out_ref,
     vis, dest, slot, off, taper, fields, v_ref, w_ref, acc, sends, recvs,
-    load_sem, a_send, a_recv, b_send, b_recv, rounds, late_sem,
+    load_sem, a_send, a_recv, b_send, b_recv, rounds,
 ):
     grp, au, vert = lax.axis_index("grp"), lax.axis_index("au"), lax.axis_index("vert")
     core, half = au % 2, au // 2
@@ -122,52 +133,54 @@
     def signal(sem, peer):
         pl.semaphore_signal(sem, inc=1, device_id=peer, device_id_type=MESH)
 
-    def near(step):
-        return (grp + step) % 4, au, vert
-
-    def across(there):
-        return there, (1 - half) * 2 + core, vert
-
-    def inside(step):
-        return (grp + step >= 0) & (grp + step < 4)
+    def ring_peer(there):
+        return there % 4, there // 4 * 2 + core, vert
+
+    def wave(place):
+        return 2 - jnp.abs(place - 2)
 
     pair = own_peer((1, 0, 0))
-    plane = [own_peer((0, 0, 1)), own_peer((0, 0, 3)), own_peer((0, 1, 0)), own_peer((0, 3, 0)), pair]
-    neighbours = len(plane) + inside(1).astype(jnp.int32) + inside(-1).astype(jnp.int32)
-
-    def signal_near(sem):
-        for peer in plane:
+    plane = []
+    for step in (1, 3):
+        plane.append((wave((x + step) % 4) < wave(x), own_peer((0, 0, step))))
+        plane.append((wave((y + step) % 4) < wave(y), own_peer((0, step, 0))))
+    plane.append((core == 0, pair))
+    before = sum(first.astype(jnp.int32) for first, _ in plane)
+
+    def signal_if(sem, wanted, peer):
+        @pl.when(wanted)
+        def _():
             signal(sem, peer)
-        for step in (1, -1):
-
-            @pl.when(inside(step))
-            def _():
-                signal(sem, near(step))
-
-    def gather(peer):
+
+    def wait_if(sem, count):
+        @pl.when(count > 0)
+        def _():
+            pl.semaphore_wait(sem, count)
+
+    def signal_plane(sem):
+        for _, peer in plane:
+            signal(sem, peer)
+
+    def gather(there):
         pltpu.make_async_remote_copy(
             src_ref=fields.at[z],
             dst_ref=fields.at[z],
             send_sem=a_send,
             recv_sem=a_recv.at[z],
-            device_id=peer,
+            device_id=ring_peer(there),
             device_id_type=MESH,
         ).start()
 
-    def gather_near(distance):
-        for step in (distance, -distance):
-
-            @pl.when(inside(step))
-            def _():
-                gather(near(step))
+    def gather_if(wanted, there):
+        @pl.when(wanted)
+        def _():
+            gather(there)
 
     barrier = pltpu.get_barrier_semaphore()
-    signal_near(barrier)
-
-    @pl.when(half == 0)
-    def _():
-        for there in range(4):
-            signal(barrier, across(there))
+    for there in range(1, RING):
+        signal_if(barrier, z < there, ring_peer(there))
+    for first, peer in plane:
+        signal_if(barrier, jnp.logical_not(first), peer)
 
     loads = [
         pltpu.make_async_copy(src, dst, load_sem.at[i])
@@ -186,17 +199,12 @@
     fields[z, 2:3, :] = (row0 - CELLS // 2).astype(jnp.float32)
     fields[z, 3:4, :] = (col0 - CELLS // 2).astype(jnp.float32)
 
-    pl.semaphore_wait(barrier, neighbours + 4 * half)
-
-    @pl.when(half == 1)
-    def _():
-        for there in range(4):
-            gather(across(there))
-        for there in range(4):
-            signal(late_sem, across(there))
-
-    gather_near(1)
-    signal_near(rounds.at[0])
+    wait_if(barrier, before + z)
+    for there in range(RING - 1):
+        gather_if(there < z, there)
+    for first, peer in plane:
+        signal_if(rounds.at[0], first, peer)
+
     position = grp * 2 + half
     first_pixel = (position * ROWS - HALF).astype(jnp.float32)
 
@@ -226,15 +234,12 @@
     line_re, line_im = line_re[0:1, :] * norm, line_im[0:1, :] * norm
     column_pixel = lane + 128 * (level % 2)
     col_re, col_im = taper_sum(taps, jnp.where(level < 2, column_pixel, -1 - column_pixel).astype(jnp.float32))
-    for distance in (2, 3):
-        pl.semaphore_wait(rounds.at[distance - 2], neighbours)
-        gather_near(distance)
-        signal_near(rounds.at[distance - 1])
+    wait_if(rounds.at[0], len(plane) - before)
+    signal_plane(rounds.at[1])
     for index in range(1, RING):
-        if index < 4:
-            source = half * 4 + (grp + index) % 4
-        else:
-            source = (1 - half) * 4 + (grp + 7 - index) % 4
+        source = ORDER[0][index - 1]
+        for place in range(1, RING):
+            source = jnp.where(z == place, ORDER[place][index - 1], source)
         pltpu.make_async_remote_copy(
             src_ref=fields.at[source],
             dst_ref=fields.at[source],
@@ -243,17 +248,12 @@
             device_id=pair,
             device_id_type=MESH,
         ).wait_recv()
+        gather_if(source > z, source)
         project(index - 1)
         phases(fields[source], first_pixel, v_ref.at[index % 2], w_ref.at[index % 2])
-        if index == 3:
-            pl.semaphore_wait(rounds.at[2], neighbours)
-            signal_near(rounds.at[3])
-
-            @pl.when(half == 0)
-            def _():
-                pl.semaphore_wait(late_sem, 4)
-                for there in range(4):
-                    gather(across(there))
+        if index < 4:
+            pl.semaphore_wait(rounds.at[index], len(plane))
+            signal_plane(rounds.at[index + 1])
 
     project(RING - 1)
     for i in range(2):
@@ -273,7 +273,7 @@
             for t in range(4):
                 sends[pl.ds(64 * t + 2 * group + i, 8, stride=8), :] = facet[8 * t : 8 * t + 8, :]
 
-    pl.semaphore_wait(rounds.at[3], neighbours)
+    pl.semaphore_wait(rounds.at[4], len(plane))
     for i, shift in enumerate(shifts):
         start = pl.multiple_of(8 * ((core + shift[0]) % 2 * 16 + own_vert(shift)), 8)
         pltpu.make_async_remote_copy(
@@ -328,8 +328,7 @@
             pltpu.SemaphoreType.DMA((RING,)),
             pltpu.SemaphoreType.DMA,
             pltpu.SemaphoreType.DMA,
-            pltpu.SemaphoreType.REGULAR((4,)),
-            pltpu.SemaphoreType.REGULAR,
+            pltpu.SemaphoreType.REGULAR((5,)),
         ],
         compiler_params=pltpu.CompilerParams(collective_id=0, has_side_effects=True),
     )(visibility.T, destination.T, tile_slot.reshape(1, -1), offsets.T, taper)

time: 22.5 us -> 22.7 us (level)
  the two profiles are of different devices: /device:TPU:1 before, /device:TPU:225 now
where the time goes in v5:
time: 22.7 us; the launch traced here: 22.6 us
  Pallas kernels  22 us (97%)
  local copies, waits for them, and re-layouts  0.6 us (3%)
    pallas_call x1, Pallas kernels, body(): pl.pallas_call(kernel, out_shape=pltpu.VMEM((2, IMG), jnp.float32), in_sp...  22 us
    unnamed x1, local copies, waits for them, and re-layouts  0.6 us

profile of v5, /device:TPU:225, one launch (start us, length us, event | category | flops | bytes accessed | tf_op | source)
XLA Modules:
  0.0 22.6 jit_solution(469151537148598320)
XLA Ops:
  0.0 22.0 %shard_map.55 = f32[2,512]{1,0:T(2,128)S(1)} custom-call(f32[2,256]{1,0:T(2,128)} %bitcast.4, s32[1,256]{1,0:T(1,128)} %bitcast.6, s32[1,256]{1,0:T(1,128)} %bitcast.7, s32[2,256]{1,0:T(2,128)} %bitcast.5, f32[8]{0:T(128)} %taper_hbm.1), custom_call_target="tpu_custom_call" | custom-call | tf_op jit(solution)/shard_map/pallas_call | solution.py:309
  22.0 0.6 %copy.7 = f32[2,512]{1,0:T(2,128)} copy(f32[2,512]{1,0:T(2,128)S(1)} %shard_map.55) | data formatting | bytes 8192

commit v6 on v5

--- a/solution.py
+++ b/solution.py
@@ -23,13 +23,13 @@
 
 ORDER = (
     (1, 2, 3, 7, 6, 5, 4),
-    (2, 3, 0, 7, 4, 6, 5),
+    (2, 3, 0, 7, 6, 4, 5),
     (3, 1, 0, 4, 5, 7, 6),
-    (4, 5, 6, 7, 2, 1, 0),
+    (2, 1, 0, 4, 5, 6, 7),
     (5, 6, 7, 3, 2, 1, 0),
-    (6, 7, 4, 3, 2, 1, 0),
-    (7, 5, 4, 3, 0, 2, 1),
-    (6, 5, 4, 0, 3, 1, 2),
+    (6, 7, 4, 3, 0, 2, 1),
+    (7, 5, 0, 4, 3, 1, 2),
+    (6, 0, 5, 1, 2, 4, 3),
 )
 
 
@@ -113,7 +113,7 @@
 def kernel(
     vis_hbm, dest_hbm, slot_hbm, off_hbm, taper_hbm, out_ref,
     vis, dest, slot, off, taper, fields, v_ref, w_ref, acc, sends, recvs,
-    load_sem, a_send, a_recv, b_send, b_recv, rounds,
+    load_sem, a_send, a_recv, b_send, b_recv, rounds, ready,
 ):
     grp, au, vert = lax.axis_index("grp"), lax.axis_index("au"), lax.axis_index("vert")
     core, half = au % 2, au // 2
@@ -202,6 +202,8 @@
     wait_if(barrier, before + z)
     for there in range(RING - 1):
         gather_if(there < z, there)
+    for there in range(RING - 1):
+        signal_if(ready.at[jnp.where(there // 4 == half, 0, 1)], there < z, ring_peer(there))
     for first, peer in plane:
         signal_if(rounds.at[0], first, peer)
 
@@ -234,9 +236,20 @@
     line_re, line_im = line_re[0:1, :] * norm, line_im[0:1, :] * norm
     column_pixel = lane + 128 * (level % 2)
     col_re, col_im = taper_sum(taps, jnp.where(level < 2, column_pixel, -1 - column_pixel).astype(jnp.float32))
+    wait_if(ready.at[0], 3 - grp)
+    for there in range(1, RING):
+        gather_if((there > z) & (there // 4 == half), there)
     wait_if(rounds.at[0], len(plane) - before)
     signal_plane(rounds.at[1])
     for index in range(1, RING):
+        if index == 4:
+
+            @pl.when(half == 0)
+            def _():
+                pl.semaphore_wait(ready.at[1], 4)
+                for there in range(4, RING):
+                    gather(there)
+
         source = ORDER[0][index - 1]
         for place in range(1, RING):
             source = jnp.where(z == place, ORDER[place][index - 1], source)
@@ -248,7 +261,6 @@
             device_id=pair,
             device_id_type=MESH,
         ).wait_recv()
-        gather_if(source > z, source)
         project(index - 1)
         phases(fields[source], first_pixel, v_ref.at[index % 2], w_ref.at[index % 2])
         if index < 4:
@@ -329,6 +341,7 @@
             pltpu.SemaphoreType.DMA,
             pltpu.SemaphoreType.DMA,
             pltpu.SemaphoreType.REGULAR((5,)),
+            pltpu.SemaphoreType.REGULAR((2,)),
         ],
         compiler_params=pltpu.CompilerParams(collective_id=0, has_side_effects=True),
     )(visibility.T, destination.T, tile_slot.reshape(1, -1), offsets.T, taper)

time: 22.7 us -> 22.5 us (level)
  no operation moved by 1% of the time
where the time goes in v6:
time: 22.5 us; the launch traced here: 22.4 us
  Pallas kernels  21.8 us (97%)
  local copies, waits for them, and re-layouts  0.6 us (3%)
    pallas_call x1, Pallas kernels, body(): pl.pallas_call(kernel, out_shape=pltpu.VMEM((2, IMG), jnp.float32), in_sp...  21.8 us
    unnamed x1, local copies, waits for them, and re-layouts  0.6 us

profile of v6, /device:TPU:225, one launch (start us, length us, event | category | flops | bytes accessed | tf_op | source)
XLA Modules:
  0.0 22.4 jit_solution(2440686784459227831)
XLA Ops:
  0.0 21.8 %shard_map.55 = f32[2,512]{1,0:T(2,128)S(1)} custom-call(f32[2,256]{1,0:T(2,128)} %bitcast.4, s32[1,256]{1,0:T(1,128)} %bitcast.6, s32[1,256]{1,0:T(1,128)} %bitcast.7, s32[2,256]{1,0:T(2,128)} %bitcast.5, f32[8]{0:T(128)} %taper_hbm.1), custom_call_target="tpu_custom_call" | custom-call | tf_op jit(solution)/shard_map/pallas_call | solution.py:321
  21.8 0.6 %copy.7 = f32[2,512]{1,0:T(2,128)} copy(f32[2,512]{1,0:T(2,128)S(1)} %shard_map.55) | data formatting | bytes 8192

commit v7 on v6

--- a/solution.py
+++ b/solution.py
@@ -236,13 +236,23 @@
     line_re, line_im = line_re[0:1, :] * norm, line_im[0:1, :] * norm
     column_pixel = lane + 128 * (level % 2)
     col_re, col_im = taper_sum(taps, jnp.where(level < 2, column_pixel, -1 - column_pixel).astype(jnp.float32))
+    def plane_round(number):
+        pl.semaphore_wait(rounds.at[number], len(plane))
+        signal_plane(rounds.at[number + 1])
+
+    wait_if(rounds.at[0], len(plane) - before)
+    signal_plane(rounds.at[1])
+
+    @pl.when(half == 0)
+    def _():
+        for number in range(1, 4):
+            plane_round(number)
+
     wait_if(ready.at[0], 3 - grp)
     for there in range(1, RING):
         gather_if((there > z) & (there // 4 == half), there)
-    wait_if(rounds.at[0], len(plane) - before)
-    signal_plane(rounds.at[1])
     for index in range(1, RING):
-        if index == 4:
+        if index == 3:
 
             @pl.when(half == 0)
             def _():
@@ -264,8 +274,10 @@
         project(index - 1)
         phases(fields[source], first_pixel, v_ref.at[index % 2], w_ref.at[index % 2])
         if index < 4:
-            pl.semaphore_wait(rounds.at[index], len(plane))
-            signal_plane(rounds.at[index + 1])
+
+            @pl.when(half == 1)
+            def _():
+                plane_round(index)
 
     project(RING - 1)
     for i in range(2):

time: 22.5 us -> 23 us (1.022)
  the two profiles are of different devices: /device:TPU:225 before, /device:TPU:193 now
where the time goes in v7:
time: 23 us; the launch traced here: 22.9 us
  Pallas kernels  22.3 us (97%)
  local copies, waits for them, and re-layouts  0.6 us (3%)
    pallas_call x1, Pallas kernels, body(): pl.pallas_call(kernel, out_shape=pltpu.VMEM((2, IMG), jnp.float32), in_sp...  22.3 us
    unnamed x1, local copies, waits for them, and re-layouts  0.6 us

profile of v7, /device:TPU:193, one launch (start us, length us, event | category | flops | bytes accessed | tf_op | source)
XLA Modules:
  0.0 22.9 jit_solution(18004434607422372895)
XLA Ops:
  0.0 22.3 %shard_map.55 = f32[2,512]{1,0:T(2,128)S(1)} custom-call(f32[2,256]{1,0:T(2,128)} %bitcast.4, s32[1,256]{1,0:T(1,128)} %bitcast.6, s32[1,256]{1,0:T(1,128)} %bitcast.7, s32[2,256]{1,0:T(2,128)} %bitcast.5, f32[8]{0:T(128)} %taper_hbm.1), custom_call_target="tpu_custom_call" | custom-call | tf_op jit(solution)/shard_map/pallas_call | solution.py:333
  22.3 0.6 %copy.7 = f32[2,512]{1,0:T(2,128)} copy(f32[2,512]{1,0:T(2,128)S(1)} %shard_map.55) | data formatting | bytes 8192

commit v8 on v6

--- a/solution.py
+++ b/solution.py
@@ -113,7 +113,7 @@
 def kernel(
     vis_hbm, dest_hbm, slot_hbm, off_hbm, taper_hbm, out_ref,
     vis, dest, slot, off, taper, fields, v_ref, w_ref, acc, sends, recvs,
-    load_sem, a_send, a_recv, b_send, b_recv, rounds, ready,
+    load_sem, a_send, a_recv, b_send, b_recv, ready, here, everyone,
 ):
     grp, au, vert = lax.axis_index("grp"), lax.axis_index("au"), lax.axis_index("vert")
     core, half = au % 2, au // 2
@@ -136,16 +136,13 @@
     def ring_peer(there):
         return there % 4, there // 4 * 2 + core, vert
 
-    def wave(place):
-        return 2 - jnp.abs(place - 2)
-
     pair = own_peer((1, 0, 0))
-    plane = []
-    for step in (1, 3):
-        plane.append((wave((x + step) % 4) < wave(x), own_peer((0, 0, step))))
-        plane.append((wave((y + step) % 4) < wave(y), own_peer((0, step, 0))))
-    plane.append((core == 0, pair))
-    before = sum(first.astype(jnp.int32) for first, _ in plane)
+    hub = grp, half * 2 + 1, 0
+    is_hub = (core == 1) & (vert == 0)
+
+    def greet_plane(sem):
+        for shift in shifts:
+            signal(sem, own_peer(shift))
 
     def signal_if(sem, wanted, peer):
         @pl.when(wanted)
@@ -156,10 +153,6 @@
         @pl.when(count > 0)
         def _():
             pl.semaphore_wait(sem, count)
-
-    def signal_plane(sem):
-        for _, peer in plane:
-            signal(sem, peer)
 
     def gather(there):
         pltpu.make_async_remote_copy(
@@ -179,8 +172,7 @@
     barrier = pltpu.get_barrier_semaphore()
     for there in range(1, RING):
         signal_if(barrier, z < there, ring_peer(there))
-    for first, peer in plane:
-        signal_if(barrier, jnp.logical_not(first), peer)
+    pl.when(is_hub)(lambda: greet_plane(barrier))
 
     loads = [
         pltpu.make_async_copy(src, dst, load_sem.at[i])
@@ -199,13 +191,12 @@
     fields[z, 2:3, :] = (row0 - CELLS // 2).astype(jnp.float32)
     fields[z, 3:4, :] = (col0 - CELLS // 2).astype(jnp.float32)
 
-    wait_if(barrier, before + z)
+    wait_if(barrier, z + jnp.where(is_hub, 0, 1))
     for there in range(RING - 1):
         gather_if(there < z, there)
     for there in range(RING - 1):
         signal_if(ready.at[jnp.where(there // 4 == half, 0, 1)], there < z, ring_peer(there))
-    for first, peer in plane:
-        signal_if(rounds.at[0], first, peer)
+    signal_if(here, jnp.logical_not(is_hub), hub)
 
     position = grp * 2 + half
     first_pixel = (position * ROWS - HALF).astype(jnp.float32)
@@ -239,10 +230,13 @@
     wait_if(ready.at[0], 3 - grp)
     for there in range(1, RING):
         gather_if((there > z) & (there // 4 == half), there)
-    wait_if(rounds.at[0], len(plane) - before)
-    signal_plane(rounds.at[1])
+    @pl.when(is_hub)
+    def _():
+        pl.semaphore_wait(here, OWN - 1)
+        greet_plane(everyone)
+
     for index in range(1, RING):
-        if index == 4:
+        if index == 3:
 
             @pl.when(half == 0)
             def _():
@@ -263,10 +257,6 @@
         ).wait_recv()
         project(index - 1)
         phases(fields[source], first_pixel, v_ref.at[index % 2], w_ref.at[index % 2])
-        if index < 4:
-            pl.semaphore_wait(rounds.at[index], len(plane))
-            signal_plane(rounds.at[index + 1])
-
     project(RING - 1)
     for i in range(2):
         rows = slice(128 * i, 128 * i + 128)
@@ -285,7 +275,7 @@
             for t in range(4):
                 sends[pl.ds(64 * t + 2 * group + i, 8, stride=8), :] = facet[8 * t : 8 * t + 8, :]
 
-    pl.semaphore_wait(rounds.at[4], len(plane))
+    wait_if(everyone, jnp.where(is_hub, 0, 1))
     for i, shift in enumerate(shifts):
         start = pl.multiple_of(8 * ((core + shift[0]) % 2 * 16 + own_vert(shift)), 8)
         pltpu.make_async_remote_copy(
@@ -340,8 +330,9 @@
             pltpu.SemaphoreType.DMA((RING,)),
             pltpu.SemaphoreType.DMA,
             pltpu.SemaphoreType.DMA,
-            pltpu.SemaphoreType.REGULAR((5,)),
             pltpu.SemaphoreType.REGULAR((2,)),
+            pltpu.SemaphoreType.REGULAR,
+            pltpu.SemaphoreType.REGULAR,
         ],
         compiler_params=pltpu.CompilerParams(collective_id=0, has_side_effects=True),
     )(visibility.T, destination.T, tile_slot.reshape(1, -1), offsets.T, taper)

time: 22.5 us -> 20.7 us (0.920)
  the two profiles are of different devices: /device:TPU:225 before, /device:TPU:1 now
where the time goes in v8:
time: 20.7 us; the launch traced here: 20.6 us
  Pallas kernels  20 us (97%)
  local copies, waits for them, and re-layouts  0.6 us (3%)
    pallas_call x1, Pallas kernels, body(): pl.pallas_call(kernel, out_shape=pltpu.VMEM((2, IMG), jnp.float32), in_sp...  20 us
    unnamed x1, local copies, waits for them, and re-layouts  0.6 us

profile of v8, /device:TPU:1, one launch (start us, length us, event | category | flops | bytes accessed | tf_op | source)
XLA Modules:
  0.0 20.6 jit_solution(5640135066914211789)
XLA Ops:
  0.0 20.0 %shard_map.55 = f32[2,512]{1,0:T(2,128)S(1)} custom-call(f32[2,256]{1,0:T(2,128)} %bitcast.4, s32[1,256]{1,0:T(1,128)} %bitcast.6, s32[1,256]{1,0:T(1,128)} %bitcast.7, s32[2,256]{1,0:T(2,128)} %bitcast.5, f32[8]{0:T(128)} %taper_hbm.1), custom_call_target="tpu_custom_call" | custom-call | tf_op jit(solution)/shard_map/pallas_call | solution.py:311
  20.0 0.6 %copy.7 = f32[2,512]{1,0:T(2,128)} copy(f32[2,512]{1,0:T(2,128)S(1)} %shard_map.55) | data formatting | bytes 8192

commit v9 on v8

--- a/solution.py
+++ b/solution.py
@@ -19,6 +19,7 @@
 OWN = 32
 ROWS = 64
 HALF = IMG // 2
+CENTRE = IMG // 4
 VIS = 256
 
 ORDER = (
@@ -79,35 +80,36 @@
 
 
 def phases(fields, first_pixel, v_ref, w_ref):
-    re, im, x, y = (fields[i : i + 1, :] for i in range(4))
-    row = rows_of((8, VIS))
+    unit = 1.0 / CELLS
+    row = rows_of((8, 128))
     rowf = row.astype(jnp.float32)
-    unit = 1.0 / CELLS
-    col = sincos((rowf + 0.5) * y * unit)
-    line = sincos(((first_pixel + 2.0 * rowf) * x - 0.5 * y) * unit)
-    power = jnp.where(row < 5, 8 << jnp.minimum(row, 4), jnp.where(row == 7, 1, 16 << jnp.maximum(row - 5, 0)))
-    turn = sincos(power.astype(jnp.float32) * jnp.where(row < 5, y, x) * unit)
-
-    def step(i):
-        return turn[0][i : i + 1, :], turn[1][i : i + 1, :]
-
-    line = times((re, im), line)
-    tiles = [stack(line, times(line, step(5)))]
-    tiles.append(times(tiles[0], step(6)))
-    tiles += [times(tile, step(7)) for tile in tiles]
-    for i, tile in enumerate(tiles):
-        for part in range(2):
-            high, low = split(tile[part])
-            w_ref[64 * part + 16 * i : 64 * part + 16 * i + 16, :] = high
-            w_ref[128 + 64 * part + 16 * i : 128 + 64 * part + 16 * i + 16, :] = low
-    tiles = [stack(col, times(col, step(0)))]
-    for level in range(1, 5):
-        tiles += [times(tile, step(level)) for tile in tiles]
-    for i, tile in enumerate(tiles):
-        for part in range(2):
-            high, low = split(tile[part])
-            v_ref[256 * part + 16 * i : 256 * part + 16 * i + 16, 0:VIS] = high
-            v_ref[256 * part + 16 * i : 256 * part + 16 * i + 16, VIS : 2 * VIS] = low
+    power = jnp.where(row < 2, 8 << jnp.minimum(row, 1), jnp.where(row == 2, CENTRE, 16 << jnp.maximum(row - 3, 0)))
+    power = jnp.where(row == 5, 1, power).astype(jnp.float32) * unit
+    for lane in range(0, VIS, 128):
+        re, im, x, y = (fields[i : i + 1, lane : lane + 128] for i in range(4))
+        col = sincos((rowf + 0.5) * (y * unit))
+        line = sincos(((first_pixel + 2.0 * rowf) * x - 0.5 * y) * unit)
+        turn = sincos(power * jnp.where(row < 3, y, x))
+        steps = [(turn[0][i : i + 1, :], turn[1][i : i + 1, :]) for i in range(6)]
+
+        def store(ref, place, value):
+            high, low = split(value)
+            ref[0, place : place + 16, lane : lane + 128] = high
+            ref[1, place : place + 16, lane : lane + 128] = low
+
+        line = times((re, im), line)
+        tiles = [stack(line, times(line, steps[3]))]
+        tiles.append(times(tiles[0], steps[4]))
+        tiles += [times(tile, steps[5]) for tile in tiles]
+        for i, tile in enumerate(tiles):
+            rr, ii, ri, ir = (tile[a] * steps[2][b] for a, b in ((0, 0), (1, 1), (0, 1), (1, 0)))
+            for place, value in ((0, rr + ii), (64, ir - ri), (128, rr - ii), (192, ri + ir)):
+                store(w_ref, place + 16 * i, value)
+        tile = stack(col, times(col, steps[0]))
+        for i in range(CENTRE // 16):
+            store(v_ref, 16 * i, tile[0])
+            store(v_ref, CENTRE + 16 * i, tile[1])
+            tile = times(tile, steps[1])
 
 
 def kernel(
@@ -202,14 +204,11 @@
     first_pixel = (position * ROWS - HALF).astype(jnp.float32)
 
     def project(index):
-        weights = w_ref[index % 2]
+        v, w = v_ref.at[index % 2], w_ref.at[index % 2]
         part = None
-        for low in range(2):
+        for a, b in ((0, 0), (0, 1), (1, 0)):
             product = lax.dot_general(
-                v_ref[index % 2, :, low * VIS : (low + 1) * VIS],
-                weights,
-                (((1,), (1,)), ((), ())),
-                preferred_element_type=jnp.float32,
+                v[a], w[b], (((1,), (1,)), ((), ())), preferred_element_type=jnp.float32
             )
             part = product if part is None else part + product
         if index == 0:
@@ -225,8 +224,8 @@
     line_re, line_im = taper_sum(taps, first_pixel + (2 * (within % 32) + within // 32).astype(jnp.float32))
     norm = 1.0 / (SUP * math.sqrt(65536))
     line_re, line_im = line_re[0:1, :] * norm, line_im[0:1, :] * norm
-    column_pixel = lane + 128 * (level % 2)
-    col_re, col_im = taper_sum(taps, jnp.where(level < 2, column_pixel, -1 - column_pixel).astype(jnp.float32))
+    centre = CENTRE * (2 * (level % 2) - 1)
+    col_re, col_im = taper_sum(taps, centre + jnp.where(level < 2, lane, -1 - lane).astype(jnp.float32))
     wait_if(ready.at[0], 3 - grp)
     for there in range(1, RING):
         gather_if((there > z) & (there // 4 == half), there)
@@ -259,10 +258,8 @@
         phases(fields[source], first_pixel, v_ref.at[index % 2], w_ref.at[index % 2])
     project(RING - 1)
     for i in range(2):
-        rows = slice(128 * i, 128 * i + 128)
-        cos_sum = acc[rows, 0:128] + acc[rows, 128:256]
-        rows = slice(256 + 128 * i, 256 + 128 * i + 128)
-        sin_sum = acc[rows, 0:128] + acc[rows, 128:256]
+        cos_sum = acc[0:128, 128 * i : 128 * i + 128]
+        sin_sum = acc[128:256, 128 * i : 128 * i + 128]
         minus = cos_sum - pltpu.roll(sin_sum, 64, 1)
         plus = pltpu.roll(cos_sum, 64, 1) + sin_sum
         mask = lanes_of((128, 128)) < 64
@@ -296,9 +293,9 @@
         total = total + recvs[i]
     mirrored = jnp.take_along_axis(total, 127 - lane, axis=1)
     for e in range(2):
-        for h in range(2):
-            out_ref[e : e + 1, 256 + 128 * h : 384 + 128 * h] = total[2 * e + h : 2 * e + h + 1, :]
-            out_ref[e : e + 1, 128 * (1 - h) : 128 * (2 - h)] = mirrored[4 + 2 * e + h : 5 + 2 * e + h, :]
+        for c in range(2):
+            out_ref[e : e + 1, 256 * c + 128 : 256 * c + 256] = total[2 * e + c : 2 * e + c + 1, :]
+            out_ref[e : e + 1, 256 * c : 256 * c + 128] = mirrored[4 + 2 * e + c : 5 + 2 * e + c, :]
     batch.wait_send()
     rest = fields.at[pl.ds(1, RING - 1)]
     pltpu.make_async_remote_copy(
@@ -320,9 +317,9 @@
             pltpu.VMEM((2, VIS), jnp.int32),
             pltpu.SMEM((SUP,), jnp.float32),
             pltpu.VMEM((RING, 4, VIS), jnp.float32),
-            pltpu.VMEM((2, IMG, 2 * VIS), jnp.bfloat16),
-            pltpu.VMEM((2, 4 * ROWS, VIS), jnp.bfloat16),
-            pltpu.VMEM((IMG, 4 * ROWS), jnp.float32),
+            pltpu.VMEM((2, 2, 2 * CENTRE, VIS), jnp.bfloat16),
+            pltpu.VMEM((2, 2, 4 * ROWS, VIS), jnp.bfloat16),
+            pltpu.VMEM((2 * CENTRE, 4 * ROWS), jnp.float32),
             pltpu.VMEM((OWN * 8, 128), jnp.float32),
             pltpu.VMEM((OWN - 1, 8, 128), jnp.float32),
             pltpu.SemaphoreType.DMA((5,)),

time: 20.7 us -> 20.4 us (0.986)
  Pallas kernels: 20 us -> 19.7 us
    pallas_call x1, Pallas kernels: 20 us -> 19.7 us  [body(): pl.pallas_call(kernel, out_shape=pltpu.VMEM((2, IMG), jnp.float32), in_sp...]
where the time goes in v9:
time: 20.4 us; the launch traced here: 20.3 us
  Pallas kernels  19.7 us (97%)
  local copies, waits for them, and re-layouts  0.6 us (3%)
    pallas_call x1, Pallas kernels, body(): pl.pallas_call(kernel, out_shape=pltpu.VMEM((2, IMG), jnp.float32), in_sp...  19.7 us
    unnamed x1, local copies, waits for them, and re-layouts  0.6 us

profile of v9, /device:TPU:1, one launch (start us, length us, event | category | flops | bytes accessed | tf_op | source)
XLA Modules:
  0.0 20.3 jit_solution(3784210694114236109)
XLA Ops:
  0.0 19.7 %shard_map.55 = f32[2,512]{1,0:T(2,128)S(1)} custom-call(f32[2,256]{1,0:T(2,128)} %bitcast.4, s32[1,256]{1,0:T(1,128)} %bitcast.6, s32[1,256]{1,0:T(1,128)} %bitcast.7, s32[2,256]{1,0:T(2,128)} %bitcast.5, f32[8]{0:T(128)} %taper_hbm.1), custom_call_target="tpu_custom_call" | custom-call | tf_op jit(solution)/shard_map/pallas_call | solution.py:308
  19.7 0.6 %copy.7 = f32[2,512]{1,0:T(2,128)} copy(f32[2,512]{1,0:T(2,128)S(1)} %shard_map.55) | data formatting | bytes 8192

commit v10 on v9

--- a/solution.py
+++ b/solution.py
@@ -82,6 +82,13 @@
 def phases(fields, first_pixel, v_ref, w_ref):
     unit = 1.0 / CELLS
     row = rows_of((8, 128))
+
+    def v_at(part, place):
+        return v_ref.at[pl.ds(2 * CENTRE * part + place, 16), :]
+
+    def w_at(part, place):
+        return w_ref.at[part, pl.ds(place, 16), :]
+
     rowf = row.astype(jnp.float32)
     power = jnp.where(row < 2, 8 << jnp.minimum(row, 1), jnp.where(row == 2, CENTRE, 16 << jnp.maximum(row - 3, 0)))
     power = jnp.where(row == 5, 1, power).astype(jnp.float32) * unit
@@ -94,8 +101,8 @@
 
         def store(ref, place, value):
             high, low = split(value)
-            ref[0, place : place + 16, lane : lane + 128] = high
-            ref[1, place : place + 16, lane : lane + 128] = low
+            ref(0, place)[:, lane : lane + 128] = high
+            ref(1, place)[:, lane : lane + 128] = low
 
         line = times((re, im), line)
         tiles = [stack(line, times(line, steps[3]))]
@@ -104,11 +111,11 @@
         for i, tile in enumerate(tiles):
             rr, ii, ri, ir = (tile[a] * steps[2][b] for a, b in ((0, 0), (1, 1), (0, 1), (1, 0)))
             for place, value in ((0, rr + ii), (64, ir - ri), (128, rr - ii), (192, ri + ir)):
-                store(w_ref, place + 16 * i, value)
+                store(w_at, place + 16 * i, value)
         tile = stack(col, times(col, steps[0]))
         for i in range(CENTRE // 16):
-            store(v_ref, 16 * i, tile[0])
-            store(v_ref, CENTRE + 16 * i, tile[1])
+            store(v_at, 16 * i, tile[0])
+            store(v_at, CENTRE + 16 * i, tile[1])
             tile = times(tile, steps[1])
 
 
@@ -136,7 +143,8 @@
         pl.semaphore_signal(sem, inc=1, device_id=peer, device_id_type=MESH)
 
     def ring_peer(there):
-        return there % 4, there // 4 * 2 + core, vert
+        other = (there // 4 + half) % 2
+        return there % 4, there // 4 * 2 + (core + other) % 2, vert
 
     pair = own_peer((1, 0, 0))
     hub = grp, half * 2 + 1, 0
@@ -171,11 +179,6 @@
         def _():
             gather(there)
 
-    barrier = pltpu.get_barrier_semaphore()
-    for there in range(1, RING):
-        signal_if(barrier, z < there, ring_peer(there))
-    pl.when(is_hub)(lambda: greet_plane(barrier))
-
     loads = [
         pltpu.make_async_copy(src, dst, load_sem.at[i])
         for i, (src, dst) in enumerate(
@@ -184,6 +187,11 @@
     ]
     for load in loads:
         load.start()
+    barrier = pltpu.get_barrier_semaphore()
+    for there in range(1, RING):
+        signal_if(barrier, z < there, ring_peer(there))
+    pl.when(is_hub)(lambda: greet_plane(barrier))
+
     for load in loads[:4]:
         load.wait()
     target, tile = dest[...], slot[...]
@@ -205,16 +213,17 @@
 
     def project(index):
         v, w = v_ref.at[index % 2], w_ref.at[index % 2]
-        part = None
-        for a, b in ((0, 0), (0, 1), (1, 0)):
-            product = lax.dot_general(
-                v[a], w[b], (((1,), (1,)), ((), ())), preferred_element_type=jnp.float32
-            )
-            part = product if part is None else part + product
+
+        def product(a, b):
+            return lax.dot_general(a, b, (((1,), (1,)), ((), ())), preferred_element_type=jnp.float32)
+
+        both, cross = product(v[...], w[0]), product(v[0 : 2 * CENTRE, :], w[1])
         if index == 0:
-            acc[...] = part
+            acc[0 : 4 * CENTRE, :] = both
+            acc[4 * CENTRE :, :] = cross
         else:
-            acc[...] += part
+            acc[0 : 4 * CENTRE, :] += both
+            acc[4 * CENTRE :, :] += cross
 
     phases(fields[z], first_pixel, v_ref.at[0], w_ref.at[0])
     loads[4].wait()
@@ -258,8 +267,10 @@
         phases(fields[source], first_pixel, v_ref.at[index % 2], w_ref.at[index % 2])
     project(RING - 1)
     for i in range(2):
-        cos_sum = acc[0:128, 128 * i : 128 * i + 128]
-        sin_sum = acc[128:256, 128 * i : 128 * i + 128]
+        cos_sum, sin_sum = (
+            sum(acc[first + 256 * part : first + 256 * part + 128, 128 * i : 128 * i + 128] for part in range(3))
+            for first in (0, 128)
+        )
         minus = cos_sum - pltpu.roll(sin_sum, 64, 1)
         plus = pltpu.roll(cos_sum, 64, 1) + sin_sum
         mask = lanes_of((128, 128)) < 64
@@ -317,9 +328,9 @@
             pltpu.VMEM((2, VIS), jnp.int32),
             pltpu.SMEM((SUP,), jnp.float32),
             pltpu.VMEM((RING, 4, VIS), jnp.float32),
-            pltpu.VMEM((2, 2, 2 * CENTRE, VIS), jnp.bfloat16),
+            pltpu.VMEM((2, 4 * CENTRE, VIS), jnp.bfloat16),
             pltpu.VMEM((2, 2, 4 * ROWS, VIS), jnp.bfloat16),
-            pltpu.VMEM((2 * CENTRE, 4 * ROWS), jnp.float32),
+            pltpu.VMEM((6 * CENTRE, 4 * ROWS), jnp.float32),
             pltpu.VMEM((OWN * 8, 128), jnp.float32),
             pltpu.VMEM((OWN - 1, 8, 128), jnp.float32),
             pltpu.SemaphoreType.DMA((5,)),

time: 20.4 us -> 19.6 us (0.961)
  Pallas kernels: 19.7 us -> 18.9 us
    pallas_call x1, Pallas kernels: 19.7 us -> 18.9 us  [body(): pl.pallas_call(kernel, out_shape=pltpu.VMEM((2, IMG), jnp.float32), in_sp...]
where the time goes in v10:
time: 19.6 us; the launch traced here: 19.5 us
  Pallas kernels  18.9 us (96%)
  local copies, waits for them, and re-layouts  0.6 us (3%)
    pallas_call x1, Pallas kernels, body(): pl.pallas_call(kernel, out_shape=pltpu.VMEM((2, IMG), jnp.float32), in_sp...  18.9 us
    unnamed x1, local copies, waits for them, and re-layouts  0.6 us

profile of v10, /device:TPU:1, one launch (start us, length us, event | category | flops | bytes accessed | tf_op | source)
XLA Modules:
  0.0 19.5 jit_solution(8475022638999240363)
XLA Ops:
  0.0 18.9 %shard_map.55 = f32[2,512]{1,0:T(2,128)S(1)} custom-call(f32[2,256]{1,0:T(2,128)} %bitcast.4, s32[1,256]{1,0:T(1,128)} %bitcast.6, s32[1,256]{1,0:T(1,128)} %bitcast.7, s32[2,256]{1,0:T(2,128)} %bitcast.5, f32[8]{0:T(128)} %taper_hbm.1), custom_call_target="tpu_custom_call" | custom-call | tf_op jit(solution)/shard_map/pallas_call | solution.py:319
  18.9 0.6 %copy.7 = f32[2,512]{1,0:T(2,128)} copy(f32[2,512]{1,0:T(2,128)S(1)} %shard_map.55) | data formatting | bytes 8192

commit v11 on v10

--- a/solution.py
+++ b/solution.py
@@ -27,10 +27,10 @@
     (2, 3, 0, 7, 6, 4, 5),
     (3, 1, 0, 4, 5, 7, 6),
     (2, 1, 0, 4, 5, 6, 7),
-    (5, 6, 7, 3, 2, 1, 0),
-    (6, 7, 4, 3, 0, 2, 1),
-    (7, 5, 0, 4, 3, 1, 2),
-    (6, 0, 5, 1, 2, 4, 3),
+    (5, 6, 3, 2, 7, 1, 0),
+    (4, 6, 7, 3, 0, 2, 1),
+    (5, 7, 4, 0, 3, 1, 2),
+    (6, 5, 0, 1, 4, 2, 3),
 )
 
 
@@ -122,7 +122,7 @@
 def kernel(
     vis_hbm, dest_hbm, slot_hbm, off_hbm, taper_hbm, out_ref,
     vis, dest, slot, off, taper, fields, v_ref, w_ref, acc, sends, recvs,
-    load_sem, a_send, a_recv, b_send, b_recv, ready, here, everyone,
+    load_sem, a_send, a_recv, b_send, b_recv, ready, chain, here, everyone,
 ):
     grp, au, vert = lax.axis_index("grp"), lax.axis_index("au"), lax.axis_index("vert")
     core, half = au % 2, au // 2
@@ -189,7 +189,7 @@
         load.start()
     barrier = pltpu.get_barrier_semaphore()
     for there in range(1, RING):
-        signal_if(barrier, z < there, ring_peer(there))
+        signal_if(barrier, (z < there) & ((half == 0) | (there == z + 1)), ring_peer(there))
     pl.when(is_hub)(lambda: greet_plane(barrier))
 
     for load in loads[:4]:
@@ -201,11 +201,15 @@
     fields[z, 2:3, :] = (row0 - CELLS // 2).astype(jnp.float32)
     fields[z, 3:4, :] = (col0 - CELLS // 2).astype(jnp.float32)
 
-    wait_if(barrier, z + jnp.where(is_hub, 0, 1))
+    lower = jnp.where(half == 0, z, 4 + jnp.minimum(grp, 1))
+    wait_if(barrier, lower + jnp.where(is_hub, 0, 1))
+    def below(there):
+        return (there < z) & ((half == 0) | (there < 4) | (there == z - 1))
+
     for there in range(RING - 1):
-        gather_if(there < z, there)
+        gather_if(below(there), there)
     for there in range(RING - 1):
-        signal_if(ready.at[jnp.where(there // 4 == half, 0, 1)], there < z, ring_peer(there))
+        signal_if(ready.at[jnp.where(there // 4 == half, 0, 1)], below(there), ring_peer(there))
     signal_if(here, jnp.logical_not(is_hub), hub)
 
     position = grp * 2 + half
@@ -235,9 +239,25 @@
     line_re, line_im = line_re[0:1, :] * norm, line_im[0:1, :] * norm
     centre = CENTRE * (2 * (level % 2) - 1)
     col_re, col_im = taper_sum(taps, centre + jnp.where(level < 2, lane, -1 - lane).astype(jnp.float32))
-    wait_if(ready.at[0], 3 - grp)
-    for there in range(1, RING):
-        gather_if((there > z) & (there // 4 == half), there)
+    @pl.when(half == 0)
+    def _():
+        wait_if(ready.at[0], 3 - grp)
+        for there in range(1, 4):
+            gather_if(there > z, there)
+
+    @pl.when(half == 1)
+    def _():
+        wait_if(ready.at[0], jnp.minimum(3 - grp, 1))
+        sides = [(grp + step >= 0) & (grp + step < 4) for step in (1, -1)]
+        for there in range(5, RING):
+            gather_if(there == z + 1, there)
+        for distance in (2, 3):
+            for step, side in zip((1, -1), sides):
+                signal_if(chain.at[distance - 2], side, ((grp + step) % 4, au, vert))
+            pl.semaphore_wait(chain.at[distance - 2], sum(side.astype(jnp.int32) for side in sides))
+            for there in range(4, RING):
+                gather_if((there == z + distance) | (there == z - distance), there)
+
     @pl.when(is_hub)
     def _():
         pl.semaphore_wait(here, OWN - 1)
@@ -339,6 +359,7 @@
             pltpu.SemaphoreType.DMA,
             pltpu.SemaphoreType.DMA,
             pltpu.SemaphoreType.REGULAR((2,)),
+            pltpu.SemaphoreType.REGULAR((2,)),
             pltpu.SemaphoreType.REGULAR,
             pltpu.SemaphoreType.REGULAR,
         ],

time: 19.6 us -> 19.2 us (0.980)
  Pallas kernels: 18.9 us -> 18.5 us
    pallas_call x1, Pallas kernels: 18.9 us -> 18.5 us  [body(): pl.pallas_call(kernel, out_shape=pltpu.VMEM((2, IMG), jnp.float32), in_sp...]
where the time goes in v11:
time: 19.2 us; the launch traced here: 19.1 us
  Pallas kernels  18.5 us (96%)
  local copies, waits for them, and re-layouts  0.6 us (3%)
    pallas_call x1, Pallas kernels, body(): pl.pallas_call(kernel, out_shape=pltpu.VMEM((2, IMG), jnp.float32), in_sp...  18.5 us
    unnamed x1, local copies, waits for them, and re-layouts  0.6 us

profile of v11, /device:TPU:1, one launch (start us, length us, event | category | flops | bytes accessed | tf_op | source)
XLA Modules:
  0.0 19.1 jit_solution(4276564013476646719)
XLA Ops:
  0.0 18.5 %shard_map.55 = f32[2,512]{1,0:T(2,128)S(1)} custom-call(f32[2,256]{1,0:T(2,128)} %bitcast.4, s32[1,256]{1,0:T(1,128)} %bitcast.6, s32[1,256]{1,0:T(1,128)} %bitcast.7, s32[2,256]{1,0:T(2,128)} %bitcast.5, f32[8]{0:T(128)} %taper_hbm.1), custom_call_target="tpu_custom_call" | custom-call | tf_op jit(solution)/shard_map/pallas_call | solution.py:339
  18.5 0.6 %copy.7 = f32[2,512]{1,0:T(2,128)} copy(f32[2,512]{1,0:T(2,128)S(1)} %shard_map.55) | data formatting | bytes 8192

commit v12 on v11

--- a/solution.py
+++ b/solution.py
@@ -119,6 +119,11 @@
             tile = times(tile, steps[1])
 
 
+def early(place):
+    core, y, x = place // 16, place // 4 % 4, place % 4
+    return min(y, 4 - y) + min(x, 4 - x) + 0.5 * (1 - core) + (2 if place == 0 else 0)
+
+
 def kernel(
     vis_hbm, dest_hbm, slot_hbm, off_hbm, taper_hbm, out_ref,
     vis, dest, slot, off, taper, fields, v_ref, w_ref, acc, sends, recvs,
@@ -153,6 +158,11 @@
     def greet_plane(sem):
         for shift in shifts:
             signal(sem, own_peer(shift))
+
+    step = 1 - 2 * core
+    before, after = z - step, z + step
+    before_exists = (half == 1) & (before >= 4) & (before < RING)
+    after_exists = (half == 1) & (after >= 4) & (after < RING)
 
     def signal_if(sem, wanted, peer):
         @pl.when(wanted)
@@ -189,7 +199,7 @@
         load.start()
     barrier = pltpu.get_barrier_semaphore()
     for there in range(1, RING):
-        signal_if(barrier, (z < there) & ((half == 0) | (there == z + 1)), ring_peer(there))
+        signal_if(barrier, ((half == 0) & (z < there)) | (after_exists & (there == after)), ring_peer(there))
     pl.when(is_hub)(lambda: greet_plane(barrier))
 
     for load in loads[:4]:
@@ -201,14 +211,14 @@
     fields[z, 2:3, :] = (row0 - CELLS // 2).astype(jnp.float32)
     fields[z, 3:4, :] = (col0 - CELLS // 2).astype(jnp.float32)
 
-    lower = jnp.where(half == 0, z, 4 + jnp.minimum(grp, 1))
+    lower = jnp.where(half == 0, z, 4 + before_exists.astype(jnp.int32))
     wait_if(barrier, lower + jnp.where(is_hub, 0, 1))
     def below(there):
-        return (there < z) & ((half == 0) | (there < 4) | (there == z - 1))
-
-    for there in range(RING - 1):
+        return ((there < z) & ((half == 0) | (there < 4))) | (before_exists & (there == before))
+
+    for there in range(RING):
         gather_if(below(there), there)
-    for there in range(RING - 1):
+    for there in range(RING):
         signal_if(ready.at[jnp.where(there // 4 == half, 0, 1)], below(there), ring_peer(there))
     signal_if(here, jnp.logical_not(is_hub), hub)
 
@@ -247,10 +257,10 @@
 
     @pl.when(half == 1)
     def _():
-        wait_if(ready.at[0], jnp.minimum(3 - grp, 1))
+        wait_if(ready.at[0], after_exists.astype(jnp.int32))
         sides = [(grp + step >= 0) & (grp + step < 4) for step in (1, -1)]
-        for there in range(5, RING):
-            gather_if(there == z + 1, there)
+        for there in range(4, RING):
+            gather_if(after_exists & (there == after), there)
         for distance in (2, 3):
             for step, side in zip((1, -1), sides):
                 signal_if(chain.at[distance - 2], side, ((grp + step) % 4, au, vert))
@@ -264,7 +274,7 @@
         greet_plane(everyone)
 
     for index in range(1, RING):
-        if index == 3:
+        if index == 4:
 
             @pl.when(half == 0)
             def _():
@@ -304,23 +314,29 @@
                 sends[pl.ds(64 * t + 2 * group + i, 8, stride=8), :] = facet[8 * t : 8 * t + 8, :]
 
     wait_if(everyone, jnp.where(is_hub, 0, 1))
-    for i, shift in enumerate(shifts):
-        start = pl.multiple_of(8 * ((core + shift[0]) % 2 * 16 + own_vert(shift)), 8)
-        pltpu.make_async_remote_copy(
-            src_ref=sends.at[pl.ds(start, 8), :],
-            dst_ref=recvs.at[i],
-            send_sem=b_send,
-            recv_sem=b_recv,
-            device_id=own_peer(shift),
-            device_id_type=MESH,
-        ).start()
-    mine = pl.multiple_of(8 * (core * 16 + vert), 8)
-    total = sends[pl.ds(mine, 8), :]
+    mine = core * 16 + vert
+    for place in sorted(range(OWN), key=early):
+        there = grp, half * 2 + place // 16, place % 16
+
+        @pl.when(mine != place)
+        def _():
+            pltpu.make_async_remote_copy(
+                src_ref=sends.at[pl.ds(8 * place, 8), :],
+                dst_ref=recvs.at[mine],
+                send_sem=b_send,
+                recv_sem=b_recv,
+                device_id=there,
+                device_id_type=MESH,
+            ).start()
+
+    recvs[mine] = sends[pl.ds(pl.multiple_of(8 * mine, 8), 8), :]
+    others = recvs.at[pl.ds(1, OWN - 1)]
     batch = pltpu.make_async_remote_copy(
-        src_ref=recvs, dst_ref=recvs, send_sem=b_send, recv_sem=b_recv, device_id=pair, device_id_type=MESH
+        src_ref=others, dst_ref=others, send_sem=b_send, recv_sem=b_recv, device_id=pair, device_id_type=MESH
     )
     batch.wait_recv()
-    for i in range(len(shifts)):
+    total = recvs[0]
+    for i in range(1, OWN):
         total = total + recvs[i]
     mirrored = jnp.take_along_axis(total, 127 - lane, axis=1)
     for e in range(2):
@@ -352,7 +368,7 @@
             pltpu.VMEM((2, 2, 4 * ROWS, VIS), jnp.bfloat16),
             pltpu.VMEM((6 * CENTRE, 4 * ROWS), jnp.float32),
             pltpu.VMEM((OWN * 8, 128), jnp.float32),
-            pltpu.VMEM((OWN - 1, 8, 128), jnp.float32),
+            pltpu.VMEM((OWN, 8, 128), jnp.float32),
             pltpu.SemaphoreType.DMA((5,)),
             pltpu.SemaphoreType.DMA,
             pltpu.SemaphoreType.DMA((RING,)),

time: 19.2 us -> 19.4 us (1.010)
  Pallas kernels: 18.5 us -> 18.7 us
    pallas_call x1, Pallas kernels: 18.5 us -> 18.7 us  [body(): pl.pallas_call(kernel, out_shape=pltpu.VMEM((2, IMG), jnp.float32), in_sp...]
where the time goes in v12:
time: 19.4 us; the launch traced here: 19.3 us
  Pallas kernels  18.7 us (96%)
  local copies, waits for them, and re-layouts  0.6 us (3%)
    pallas_call x1, Pallas kernels, body(): pl.pallas_call(kernel, out_shape=pltpu.VMEM((2, IMG), jnp.float32), in_sp...  18.7 us
    unnamed x1, local copies, waits for them, and re-layouts  0.6 us

profile of v12, /device:TPU:1, one launch (start us, length us, event | category | flops | bytes accessed | tf_op | source)
XLA Modules:
  0.0 19.3 jit_solution(14839038144983006526)
XLA Ops:
  0.0 18.7 %shard_map.55 = f32[2,512]{1,0:T(2,128)S(1)} custom-call(f32[2,256]{1,0:T(2,128)} %bitcast.4, s32[1,256]{1,0:T(1,128)} %bitcast.6, s32[1,256]{1,0:T(1,128)} %bitcast.7, s32[2,256]{1,0:T(2,128)} %bitcast.5, f32[8]{0:T(128)} %taper_hbm.1), custom_call_target="tpu_custom_call" | custom-call | tf_op jit(solution)/shard_map/pallas_call | solution.py:355
  18.7 0.6 %copy.7 = f32[2,512]{1,0:T(2,128)} copy(f32[2,512]{1,0:T(2,128)S(1)} %shard_map.55) | data formatting | bytes 8192

commit v13 on v12

--- a/solution.py
+++ b/solution.py
@@ -84,10 +84,10 @@
     row = rows_of((8, 128))
 
     def v_at(part, place):
-        return v_ref.at[pl.ds(2 * CENTRE * part + place, 16), :]
+        return v_ref.at[part, pl.ds(place, 16), :]
 
     def w_at(part, place):
-        return w_ref.at[part, pl.ds(place, 16), :]
+        return w_ref.at[pl.ds(4 * ROWS * part + place, 16), :]
 
     rowf = row.astype(jnp.float32)
     power = jnp.where(row < 2, 8 << jnp.minimum(row, 1), jnp.where(row == 2, CENTRE, 16 << jnp.maximum(row - 3, 0)))
@@ -126,7 +126,7 @@
 
 def kernel(
     vis_hbm, dest_hbm, slot_hbm, off_hbm, taper_hbm, out_ref,
-    vis, dest, slot, off, taper, fields, v_ref, w_ref, acc, sends, recvs,
+    vis, dest, slot, off, taper, fields, v_ref, w_ref, acc, tt, sends, recvs,
     load_sem, a_send, a_recv, b_send, b_recv, ready, chain, here, everyone,
 ):
     grp, au, vert = lax.axis_index("grp"), lax.axis_index("au"), lax.axis_index("vert")
@@ -231,24 +231,27 @@
         def product(a, b):
             return lax.dot_general(a, b, (((1,), (1,)), ((), ())), preferred_element_type=jnp.float32)
 
-        both, cross = product(v[...], w[0]), product(v[0 : 2 * CENTRE, :], w[1])
+        both, cross = product(w[...], v[0]), product(w[0 : 4 * ROWS, :], v[1])
         if index == 0:
-            acc[0 : 4 * CENTRE, :] = both
-            acc[4 * CENTRE :, :] = cross
+            acc[0 : 8 * ROWS, :] = both
+            acc[8 * ROWS :, :] = cross
         else:
-            acc[0 : 4 * CENTRE, :] += both
-            acc[4 * CENTRE :, :] += cross
+            acc[0 : 8 * ROWS, :] += both
+            acc[8 * ROWS :, :] += cross
 
     phases(fields[z], first_pixel, v_ref.at[0], w_ref.at[0])
     loads[4].wait()
     taps = [taper[i] for i in range(SUP)]
     lane, level = lanes_of((8, 128)), rows_of((8, 128))
-    within = lane % 64
-    line_re, line_im = taper_sum(taps, first_pixel + (2 * (within % 32) + within // 32).astype(jnp.float32))
+    line_row = rows_of((ROWS, 128))
+    line = taper_sum(taps, first_pixel + (2 * (line_row % 32) + line_row // 32).astype(jnp.float32))
+    centre = CENTRE * (2 * (level % 2) - 1)
+    columns = taper_sum(taps, centre + jnp.where(level < 2, lane, -1 - lane).astype(jnp.float32))
     norm = 1.0 / (SUP * math.sqrt(65536))
-    line_re, line_im = line_re[0:1, :] * norm, line_im[0:1, :] * norm
-    centre = CENTRE * (2 * (level % 2) - 1)
-    col_re, col_im = taper_sum(taps, centre + jnp.where(level < 2, lane, -1 - lane).astype(jnp.float32))
+    for i in range(4):
+        pair_re, pair_im = times(line, (columns[0][i : i + 1, :] * norm, columns[1][i : i + 1, :] * norm))
+        tt[i, 0] = pair_re
+        tt[i, 1] = pair_im
     @pl.when(half == 0)
     def _():
         wait_if(ready.at[0], 3 - grp)
@@ -274,7 +277,7 @@
         greet_plane(everyone)
 
     for index in range(1, RING):
-        if index == 4:
+        if index == 3:
 
             @pl.when(half == 0)
             def _():
@@ -296,22 +299,20 @@
         project(index - 1)
         phases(fields[source], first_pixel, v_ref.at[index % 2], w_ref.at[index % 2])
     project(RING - 1)
-    for i in range(2):
-        cos_sum, sin_sum = (
-            sum(acc[first + 256 * part : first + 256 * part + 128, 128 * i : 128 * i + 128] for part in range(3))
-            for first in (0, 128)
+    for c in range(2):
+        re_cos, re_sin, im_cos, im_sin = (
+            sum(acc[first + 4 * ROWS * i : first + 4 * ROWS * i + ROWS, place : place + 128] for i in range(3))
+            for first in (128 * c, 128 * c + ROWS)
+            for place in (0, 128)
         )
-        minus = cos_sum - pltpu.roll(sin_sum, 64, 1)
-        plus = pltpu.roll(cos_sum, 64, 1) + sin_sum
-        mask = lanes_of((128, 128)) < 64
-        real, imag = jnp.where(mask, minus, plus), jnp.where(mask, plus, minus)
-        real, imag = (line_re * real - line_im * imag).T, (line_re * imag + line_im * real).T
-        for group in range(4):
-            part = slice(32 * group, 32 * group + 32)
-            tap = slice(group // 2 * 2 + i, group // 2 * 2 + i + 1)
-            facet = col_re[tap, :] * real[part, :] - col_im[tap, :] * imag[part, :]
-            for t in range(4):
-                sends[pl.ds(64 * t + 2 * group + i, 8, stride=8), :] = facet[8 * t : 8 * t + 8, :]
+        sides = (re_cos - im_sin, im_cos + re_sin), (re_cos + im_sin, im_cos - re_sin)
+        for side, (real, imag) in enumerate(sides):
+            facet = tt[2 * side + c, 0] * real - tt[2 * side + c, 1] * imag
+            for e in range(2):
+                for t in range(4):
+                    sends[pl.ds(64 * t + 4 * side + 2 * e + c, 8, stride=8), :] = facet[
+                        32 * e + 8 * t : 32 * e + 8 * t + 8, :
+                    ]
 
     wait_if(everyone, jnp.where(is_hub, 0, 1))
     mine = core * 16 + vert
@@ -364,9 +365,10 @@
             pltpu.VMEM((2, VIS), jnp.int32),
             pltpu.SMEM((SUP,), jnp.float32),
             pltpu.VMEM((RING, 4, VIS), jnp.float32),
-            pltpu.VMEM((2, 4 * CENTRE, VIS), jnp.bfloat16),
-            pltpu.VMEM((2, 2, 4 * ROWS, VIS), jnp.bfloat16),
-            pltpu.VMEM((6 * CENTRE, 4 * ROWS), jnp.float32),
+            pltpu.VMEM((2, 2, 2 * CENTRE, VIS), jnp.bfloat16),
+            pltpu.VMEM((2, 8 * ROWS, VIS), jnp.bfloat16),
+            pltpu.VMEM((12 * ROWS, 2 * CENTRE), jnp.float32),
+            pltpu.VMEM((4, 2, ROWS, 128), jnp.float32),
             pltpu.VMEM((OWN * 8, 128), jnp.float32),
             pltpu.VMEM((OWN, 8, 128), jnp.float32),
             pltpu.SemaphoreType.DMA((5,)),

time: 19.4 us -> 19 us (0.979)
  Pallas kernels: 18.7 us -> 18.3 us
    pallas_call x1, Pallas kernels: 18.7 us -> 18.3 us  [body(): pl.pallas_call(kernel, out_shape=pltpu.VMEM((2, IMG), jnp.float32), in_sp...]
where the time goes in v13:
time: 19 us; the launch traced here: 18.9 us
  Pallas kernels  18.3 us (96%)
  local copies, waits for them, and re-layouts  0.6 us (3%)
    pallas_call x1, Pallas kernels, body(): pl.pallas_call(kernel, out_shape=pltpu.VMEM((2, IMG), jnp.float32), in_sp...  18.3 us
    unnamed x1, local copies, waits for them, and re-layouts  0.6 us

profile of v13, /device:TPU:1, one launch (start us, length us, event | category | flops | bytes accessed | tf_op | source)
XLA Modules:
  0.0 18.9 jit_solution(1265050020809169324)
XLA Ops:
  0.0 18.3 %shard_map.55 = f32[2,512]{1,0:T(2,128)S(1)} custom-call(f32[2,256]{1,0:T(2,128)} %bitcast.4, s32[1,256]{1,0:T(1,128)} %bitcast.6, s32[1,256]{1,0:T(1,128)} %bitcast.7, s32[2,256]{1,0:T(2,128)} %bitcast.5, f32[8]{0:T(128)} %taper_hbm.1), custom_call_target="tpu_custom_call" | custom-call | tf_op jit(solution)/shard_map/pallas_call | solution.py:356
  18.3 0.6 %copy.7 = f32[2,512]{1,0:T(2,128)} copy(f32[2,512]{1,0:T(2,128)S(1)} %shard_map.55) | data formatting | bytes 8192

commit v14 on v13

--- a/solution.py
+++ b/solution.py
@@ -23,10 +23,18 @@
 VIS = 256
 
 ORDER = (
-    (1, 2, 3, 7, 6, 5, 4),
-    (2, 3, 0, 7, 6, 4, 5),
-    (3, 1, 0, 4, 5, 7, 6),
-    (2, 1, 0, 4, 5, 6, 7),
+    (1, 2, 3, 6, 5, 7),
+    (2, 3, 0, 7, 6, 5),
+    (3, 1, 0, 5, 7, 6),
+    (2, 1, 0, 5, 6, 7),
+    (5, 6, 3, 2, 7, 1, 0),
+    (4, 6, 7, 3, 0, 2, 1),
+    (5, 7, 4, 0, 3, 1, 2),
+    (6, 5, 0, 1, 4, 2, 3),
+    (1, 2, 3, 7, 6, 8, 5, 4),
+    (2, 3, 0, 7, 8, 6, 4, 5),
+    (3, 1, 0, 8, 4, 5, 7, 6),
+    (2, 1, 0, 8, 4, 5, 6, 7),
     (5, 6, 3, 2, 7, 1, 0),
     (4, 6, 7, 3, 0, 2, 1),
     (5, 7, 4, 0, 3, 1, 2),
@@ -174,13 +182,18 @@
         def _():
             pl.semaphore_wait(sem, count)
 
+    turned = (z == 4) & (core == 1)
+
     def gather(there):
+        straight = turned & (there < 4)
+        place, target, line = ring_peer(there)
+        slot_there = jnp.where(straight, RING, z)
         pltpu.make_async_remote_copy(
             src_ref=fields.at[z],
-            dst_ref=fields.at[z],
+            dst_ref=fields.at[slot_there],
             send_sem=a_send,
-            recv_sem=a_recv.at[z],
-            device_id=ring_peer(there),
+            recv_sem=a_recv.at[slot_there],
+            device_id=(place, target + straight.astype(jnp.int32), line),
             device_id_type=MESH,
         ).start()
 
@@ -200,6 +213,7 @@
     barrier = pltpu.get_barrier_semaphore()
     for there in range(1, RING):
         signal_if(barrier, ((half == 0) & (z < there)) | (after_exists & (there == after)), ring_peer(there))
+    signal_if(barrier, (half == 0) & (core == 1), (0, 3, vert))
     pl.when(is_hub)(lambda: greet_plane(barrier))
 
     for load in loads[:4]:
@@ -211,7 +225,7 @@
     fields[z, 2:3, :] = (row0 - CELLS // 2).astype(jnp.float32)
     fields[z, 3:4, :] = (col0 - CELLS // 2).astype(jnp.float32)
 
-    lower = jnp.where(half == 0, z, 4 + before_exists.astype(jnp.int32))
+    lower = jnp.where(half == 0, z, 4 + before_exists.astype(jnp.int32) + jnp.where(turned, 4, 0))
     wait_if(barrier, lower + jnp.where(is_hub, 0, 1))
     def below(there):
         return ((there < z) & ((half == 0) | (there < 4))) | (before_exists & (there == before))
@@ -225,21 +239,21 @@
     position = grp * 2 + half
     first_pixel = (position * ROWS - HALF).astype(jnp.float32)
 
-    def project(index):
-        v, w = v_ref.at[index % 2], w_ref.at[index % 2]
+    def project(buffer, first=False):
+        v, w = v_ref.at[buffer], w_ref.at[buffer]
 
         def product(a, b):
             return lax.dot_general(a, b, (((1,), (1,)), ((), ())), preferred_element_type=jnp.float32)
 
         both, cross = product(w[...], v[0]), product(w[0 : 4 * ROWS, :], v[1])
-        if index == 0:
+        if first:
             acc[0 : 8 * ROWS, :] = both
             acc[8 * ROWS :, :] = cross
         else:
             acc[0 : 8 * ROWS, :] += both
             acc[8 * ROWS :, :] += cross
 
-    phases(fields[z], first_pixel, v_ref.at[0], w_ref.at[0])
+    phases(fields.at[z], first_pixel, v_ref.at[0], w_ref.at[0])
     loads[4].wait()
     taps = [taper[i] for i in range(SUP)]
     lane, level = lanes_of((8, 128)), rows_of((8, 128))
@@ -276,18 +290,13 @@
         pl.semaphore_wait(here, OWN - 1)
         greet_plane(everyone)
 
-    for index in range(1, RING):
-        if index == 3:
-
-            @pl.when(half == 0)
-            def _():
-                pl.semaphore_wait(ready.at[1], 4)
-                for there in range(4, RING):
-                    gather(there)
-
-        source = ORDER[0][index - 1]
-        for place in range(1, RING):
-            source = jnp.where(z == place, ORDER[place][index - 1], source)
+    count = jnp.where(half == 1, 7, jnp.where(core == 1, 8, 6))
+
+    def take(index):
+        source = 0
+        for place, order in enumerate(ORDER):
+            if index <= len(order):
+                source = jnp.where(z + RING * core == place, order[index - 1], source)
         pltpu.make_async_remote_copy(
             src_ref=fields.at[source],
             dst_ref=fields.at[source],
@@ -296,9 +305,24 @@
             device_id=pair,
             device_id_type=MESH,
         ).wait_recv()
-        project(index - 1)
-        phases(fields[source], first_pixel, v_ref.at[index % 2], w_ref.at[index % 2])
-    project(RING - 1)
+        project((index - 1) % 2, index == 1)
+        phases(fields.at[source], first_pixel, v_ref.at[index % 2], w_ref.at[index % 2])
+
+    for index in range(1, RING + 1):
+        if index == 3:
+
+            @pl.when(half == 0)
+            def _():
+                pl.semaphore_wait(ready.at[1], 4)
+                for there in range(4, RING):
+                    gather(there)
+
+        if index < 7:
+            take(index)
+        else:
+            pl.when(count >= index)(lambda: take(index))
+
+    project(count % 2)
     for c in range(2):
         re_cos, re_sin, im_cos, im_sin = (
             sum(acc[first + 4 * ROWS * i : first + 4 * ROWS * i + ROWS, place : place + 128] for i in range(3))
@@ -364,7 +388,7 @@
             pltpu.VMEM((1, VIS), jnp.int32),
             pltpu.VMEM((2, VIS), jnp.int32),
             pltpu.SMEM((SUP,), jnp.float32),
-            pltpu.VMEM((RING, 4, VIS), jnp.float32),
+            pltpu.VMEM((RING + 1, 4, VIS), jnp.float32),
             pltpu.VMEM((2, 2, 2 * CENTRE, VIS), jnp.bfloat16),
             pltpu.VMEM((2, 8 * ROWS, VIS), jnp.bfloat16),
             pltpu.VMEM((12 * ROWS, 2 * CENTRE), jnp.float32),
@@ -373,7 +397,7 @@
             pltpu.VMEM((OWN, 8, 128), jnp.float32),
             pltpu.SemaphoreType.DMA((5,)),
             pltpu.SemaphoreType.DMA,
-            pltpu.SemaphoreType.DMA((RING,)),
+            pltpu.SemaphoreType.DMA((RING + 1,)),
             pltpu.SemaphoreType.DMA,
             pltpu.SemaphoreType.DMA,
             pltpu.SemaphoreType.REGULAR((2,)),

time: 19 us -> 18.8 us (0.989)
  Pallas kernels: 18.3 us -> 18.1 us
    pallas_call x1, Pallas kernels: 18.3 us -> 18.1 us  [body(): pl.pallas_call(kernel, out_shape=pltpu.VMEM((2, IMG), jnp.float32), in_sp...]
where the time goes in v14:
time: 18.8 us; the launch traced here: 18.7 us
  Pallas kernels  18.1 us (96%)
  local copies, waits for them, and re-layouts  0.6 us (3%)
    pallas_call x1, Pallas kernels, body(): pl.pallas_call(kernel, out_shape=pltpu.VMEM((2, IMG), jnp.float32), in_sp...  18.1 us
    unnamed x1, local copies, waits for them, and re-layouts  0.6 us

profile of v14, /device:TPU:1, one launch (start us, length us, event | category | flops | bytes accessed | tf_op | source)
XLA Modules:
  0.0 18.7 jit_solution(6961096731518310333)
XLA Ops:
  0.0 18.1 %shard_map.55 = f32[2,512]{1,0:T(2,128)S(1)} custom-call(f32[2,256]{1,0:T(2,128)} %bitcast.4, s32[1,256]{1,0:T(1,128)} %bitcast.6, s32[1,256]{1,0:T(1,128)} %bitcast.7, s32[2,256]{1,0:T(2,128)} %bitcast.5, f32[8]{0:T(128)} %taper_hbm.1), custom_call_target="tpu_custom_call" | custom-call | tf_op jit(solution)/shard_map/pallas_call | solution.py:380
  18.1 0.6 %copy.7 = f32[2,512]{1,0:T(2,128)} copy(f32[2,512]{1,0:T(2,128)S(1)} %shard_map.55) | data formatting | bytes 8192

commit v15 on v14

--- a/solution.py
+++ b/solution.py
@@ -290,8 +290,6 @@
         pl.semaphore_wait(here, OWN - 1)
         greet_plane(everyone)
 
-    count = jnp.where(half == 1, 7, jnp.where(core == 1, 8, 6))
-
     def take(index):
         source = 0
         for place, order in enumerate(ORDER):
@@ -308,7 +306,12 @@
         project((index - 1) % 2, index == 1)
         phases(fields.at[source], first_pixel, v_ref.at[index % 2], w_ref.at[index % 2])
 
-    for index in range(1, RING + 1):
+    def rest_of(count):
+        for index in range(4, count + 1):
+            take(index)
+        project(count % 2)
+
+    for index in range(1, 4):
         if index == 3:
 
             @pl.when(half == 0)
@@ -317,12 +320,10 @@
                 for there in range(4, RING):
                     gather(there)
 
-        if index < 7:
-            take(index)
-        else:
-            pl.when(count >= index)(lambda: take(index))
-
-    project(count % 2)
+        take(index)
+    pl.when((half == 0) & (core == 0))(lambda: rest_of(6))
+    pl.when(half == 1)(lambda: rest_of(7))
+    pl.when((half == 0) & (core == 1))(lambda: rest_of(8))
     for c in range(2):
         re_cos, re_sin, im_cos, im_sin = (
             sum(acc[first + 4 * ROWS * i : first + 4 * ROWS * i + ROWS, place : place + 128] for i in range(3))

time: 18.8 us -> 18.6 us (0.989)
  Pallas kernels: 18.1 us -> 17.9 us
    pallas_call x1, Pallas kernels: 18.1 us -> 17.9 us  [body(): pl.pallas_call(kernel, out_shape=pltpu.VMEM((2, IMG), jnp.float32), in_sp...]
where the time goes in v15:
time: 18.6 us; the launch traced here: 18.5 us
  Pallas kernels  17.9 us (96%)
  local copies, waits for them, and re-layouts  0.6 us (3%)
    pallas_call x1, Pallas kernels, body(): pl.pallas_call(kernel, out_shape=pltpu.VMEM((2, IMG), jnp.float32), in_sp...  17.9 us
    unnamed x1, local copies, waits for them, and re-layouts  0.6 us

profile of v15, /device:TPU:1, one launch (start us, length us, event | category | flops | bytes accessed | tf_op | source)
XLA Modules:
  0.0 18.5 jit_solution(17373390307669402734)
XLA Ops:
  0.0 17.9 %shard_map.55 = f32[2,512]{1,0:T(2,128)S(1)} custom-call(f32[2,256]{1,0:T(2,128)} %bitcast.4, s32[1,256]{1,0:T(1,128)} %bitcast.6, s32[1,256]{1,0:T(1,128)} %bitcast.7, s32[2,256]{1,0:T(2,128)} %bitcast.5, f32[8]{0:T(128)} %taper_hbm.1), custom_call_target="tpu_custom_call" | custom-call | tf_op jit(solution)/shard_map/pallas_call | solution.py:381
  17.9 0.6 %copy.7 = f32[2,512]{1,0:T(2,128)} copy(f32[2,512]{1,0:T(2,128)S(1)} %shard_map.55) | data formatting | bytes 8192

commit v16 on v15

--- a/solution.py
+++ b/solution.py
@@ -307,19 +307,16 @@
         phases(fields.at[source], first_pixel, v_ref.at[index % 2], w_ref.at[index % 2])
 
     def rest_of(count):
-        for index in range(4, count + 1):
-            take(index)
-        project(count % 2)
-
-    for index in range(1, 4):
-        if index == 3:
-
-            @pl.when(half == 0)
-            def _():
+        for index in range(3, count + 1):
+            if index == 3 and count != 7:
                 pl.semaphore_wait(ready.at[1], 4)
                 for there in range(4, RING):
                     gather(there)
 
+            take(index)
+        project(count % 2)
+
+    for index in range(1, 3):
         take(index)
     pl.when((half == 0) & (core == 0))(lambda: rest_of(6))
     pl.when(half == 1)(lambda: rest_of(7))

time: 18.6 us -> 18.5 us (level)
  no operation moved by 1% of the time
where the time goes in v16:
time: 18.5 us; the launch traced here: 18.4 us
  Pallas kernels  17.8 us (96%)
  local copies, waits for them, and re-layouts  0.6 us (3%)
    pallas_call x1, Pallas kernels, body(): pl.pallas_call(kernel, out_shape=pltpu.VMEM((2, IMG), jnp.float32), in_sp...  17.8 us
    unnamed x1, local copies, waits for them, and re-layouts  0.6 us

profile of v16, /device:TPU:1, one launch (start us, length us, event | category | flops | bytes accessed | tf_op | source)
XLA Modules:
  0.0 18.4 jit_solution(6535235452388378693)
XLA Ops:
  0.0 17.8 %shard_map.55 = f32[2,512]{1,0:T(2,128)S(1)} custom-call(f32[2,256]{1,0:T(2,128)} %bitcast.4, s32[1,256]{1,0:T(1,128)} %bitcast.6, s32[1,256]{1,0:T(1,128)} %bitcast.7, s32[2,256]{1,0:T(2,128)} %bitcast.5, f32[8]{0:T(128)} %taper_hbm.1), custom_call_target="tpu_custom_call" | custom-call | tf_op jit(solution)/shard_map/pallas_call | solution.py:378
  17.8 0.6 %copy.7 = f32[2,512]{1,0:T(2,128)} copy(f32[2,512]{1,0:T(2,128)S(1)} %shard_map.55) | data formatting | bytes 8192

commit v17 on v16

--- a/solution.py
+++ b/solution.py
@@ -27,17 +27,17 @@
     (2, 3, 0, 7, 6, 5),
     (3, 1, 0, 5, 7, 6),
     (2, 1, 0, 5, 6, 7),
-    (5, 6, 3, 2, 7, 1, 0),
-    (4, 6, 7, 3, 0, 2, 1),
-    (5, 7, 4, 0, 3, 1, 2),
+    (5, 6, 7, 2, 1, 3, 0),
+    (4, 6, 7, 0, 2, 1, 3),
+    (5, 7, 4, 0, 1, 2, 3),
     (6, 5, 0, 1, 4, 2, 3),
     (1, 2, 3, 7, 6, 8, 5, 4),
     (2, 3, 0, 7, 8, 6, 4, 5),
     (3, 1, 0, 8, 4, 5, 7, 6),
     (2, 1, 0, 8, 4, 5, 6, 7),
-    (5, 6, 3, 2, 7, 1, 0),
-    (4, 6, 7, 3, 0, 2, 1),
-    (5, 7, 4, 0, 3, 1, 2),
+    (5, 6, 7, 2, 1, 3, 0),
+    (4, 6, 7, 0, 2, 1, 3),
+    (5, 7, 4, 0, 1, 2, 3),
     (6, 5, 0, 1, 4, 2, 3),
 )
 
@@ -112,6 +112,11 @@
             ref(0, place)[:, lane : lane + 128] = high
             ref(1, place)[:, lane : lane + 128] = low
 
+        tile = stack(col, times(col, steps[0]))
+        for i in range(CENTRE // 16):
+            store(v_at, 16 * i, tile[0])
+            store(v_at, CENTRE + 16 * i, tile[1])
+            tile = times(tile, steps[1])
         line = times((re, im), line)
         tiles = [stack(line, times(line, steps[3]))]
         tiles.append(times(tiles[0], steps[4]))
@@ -120,11 +125,6 @@
             rr, ii, ri, ir = (tile[a] * steps[2][b] for a, b in ((0, 0), (1, 1), (0, 1), (1, 0)))
             for place, value in ((0, rr + ii), (64, ir - ri), (128, rr - ii), (192, ri + ir)):
                 store(w_at, place + 16 * i, value)
-        tile = stack(col, times(col, steps[0]))
-        for i in range(CENTRE // 16):
-            store(v_at, 16 * i, tile[0])
-            store(v_at, CENTRE + 16 * i, tile[1])
-            tile = times(tile, steps[1])
 
 
 def early(place):

time: 18.5 us -> 18.4 us (level)
  no operation moved by 1% of the time
where the time goes in v17:
time: 18.4 us; the launch traced here: 18.3 us
  Pallas kernels  17.7 us (96%)
  local copies, waits for them, and re-layouts  0.6 us (3%)
    pallas_call x1, Pallas kernels, body(): pl.pallas_call(kernel, out_shape=pltpu.VMEM((2, IMG), jnp.float32), in_sp...  17.7 us
    unnamed x1, local copies, waits for them, and re-layouts  0.6 us

profile of v17, /device:TPU:1, one launch (start us, length us, event | category | flops | bytes accessed | tf_op | source)
XLA Modules:
  0.0 18.3 jit_solution(18284350152795415872)
XLA Ops:
  0.0 17.7 %shard_map.55 = f32[2,512]{1,0:T(2,128)S(1)} custom-call(f32[2,256]{1,0:T(2,128)} %bitcast.4, s32[1,256]{1,0:T(1,128)} %bitcast.6, s32[1,256]{1,0:T(1,128)} %bitcast.7, s32[2,256]{1,0:T(2,128)} %bitcast.5, f32[8]{0:T(128)} %taper_hbm.1), custom_call_target="tpu_custom_call" | custom-call | tf_op jit(solution)/shard_map/pallas_call | solution.py:378
  17.7 0.6 %copy.7 = f32[2,512]{1,0:T(2,128)} copy(f32[2,512]{1,0:T(2,128)S(1)} %shard_map.55) | data formatting | bytes 8192

commit v18 on v17

--- a/solution.py
+++ b/solution.py
@@ -125,11 +125,6 @@
             rr, ii, ri, ir = (tile[a] * steps[2][b] for a, b in ((0, 0), (1, 1), (0, 1), (1, 0)))
             for place, value in ((0, rr + ii), (64, ir - ri), (128, rr - ii), (192, ri + ir)):
                 store(w_at, place + 16 * i, value)
-
-
-def early(place):
-    core, y, x = place // 16, place // 4 % 4, place % 4
-    return min(y, 4 - y) + min(x, 4 - x) + 0.5 * (1 - core) + (2 if place == 0 else 0)
 
 
 def kernel(
@@ -338,20 +333,16 @@
 
     wait_if(everyone, jnp.where(is_hub, 0, 1))
     mine = core * 16 + vert
-    for place in sorted(range(OWN), key=early):
-        there = grp, half * 2 + place // 16, place % 16
-
-        @pl.when(mine != place)
-        def _():
-            pltpu.make_async_remote_copy(
-                src_ref=sends.at[pl.ds(8 * place, 8), :],
-                dst_ref=recvs.at[mine],
-                send_sem=b_send,
-                recv_sem=b_recv,
-                device_id=there,
-                device_id_type=MESH,
-            ).start()
-
+    for shift in shifts:
+        start = pl.multiple_of(8 * ((core + shift[0]) % 2 * 16 + own_vert(shift)), 8)
+        pltpu.make_async_remote_copy(
+            src_ref=sends.at[pl.ds(start, 8), :],
+            dst_ref=recvs.at[mine],
+            send_sem=b_send,
+            recv_sem=b_recv,
+            device_id=own_peer(shift),
+            device_id_type=MESH,
+        ).start()
     recvs[mine] = sends[pl.ds(pl.multiple_of(8 * mine, 8), 8), :]
     others = recvs.at[pl.ds(1, OWN - 1)]
     batch = pltpu.make_async_remote_copy(

time: 18.4 us -> 19 us (1.033)
  Pallas kernels: 17.7 us -> 18.3 us
    pallas_call x1, Pallas kernels: 17.7 us -> 18.3 us  [body(): pl.pallas_call(kernel, out_shape=pltpu.VMEM((2, IMG), jnp.float32), in_sp...]
where the time goes in v18:
time: 19 us; the launch traced here: 18.9 us
  Pallas kernels  18.3 us (96%)
  local copies, waits for them, and re-layouts  0.6 us (3%)
    pallas_call x1, Pallas kernels, body(): pl.pallas_call(kernel, out_shape=pltpu.VMEM((2, IMG), jnp.float32), in_sp...  18.3 us
    unnamed x1, local copies, waits for them, and re-layouts  0.6 us

profile of v18, /device:TPU:1, one launch (start us, length us, event | category | flops | bytes accessed | tf_op | source)
XLA Modules:
  0.0 18.9 jit_solution(13255196900356375785)
XLA Ops:
  0.0 18.3 %shard_map.55 = f32[2,512]{1,0:T(2,128)S(1)} custom-call(f32[2,256]{1,0:T(2,128)} %bitcast.4, s32[1,256]{1,0:T(1,128)} %bitcast.6, s32[1,256]{1,0:T(1,128)} %bitcast.7, s32[2,256]{1,0:T(2,128)} %bitcast.5, f32[8]{0:T(128)} %taper_hbm.1), custom_call_target="tpu_custom_call" | custom-call | tf_op jit(solution)/shard_map/pallas_call | solution.py:369
  18.3 0.6 %copy.7 = f32[2,512]{1,0:T(2,128)} copy(f32[2,512]{1,0:T(2,128)S(1)} %shard_map.55) | data formatting | bytes 8192
